TPU v7x, 32 devices: a 4x4x1 block of a 4x4x8 slice. The times are simulated.
32 devices in a mesh: batch: 1 (over z), tp: 4 (over y), sp: 8 (over x, core).
Axes of the slice: x: 4, y: 4, z: 1, core: 2. Of those that a mesh axis runs over, the one named last changes fastest.
The devices are a block of a 4x4x8 slice.
Arguments:
- tokens: bfloat16 [16384, 2560], P(('batch', 'sp'))
- glob_pos: int32 [512], P('batch')
- rel_bias: float32 [20, 513], P('tp')
- w_query: bfloat16 [2560, 2560], P(None, 'tp')
- w_key: bfloat16 [2560, 2560], P(None, 'tp')
- w_value: bfloat16 [2560, 2560], P(None, 'tp')
- w_query_glob: bfloat16 [2560, 2560], P(None, 'tp')
- w_out: bfloat16 [2560, 2560], P('tp')
- w_up: bfloat16 [2560, 10240], P(None, 'tp')
- w_down: bfloat16 [10240, 2560], P('tp')
Outputs:
- output: bfloat16 [16384, 2560], P(('batch', 'sp'))
All inputs are finite; a program needn't handle non-finite values.
Results may differ from a plain program's by a relative error of at most 0.0114115.
Values are sent between devices in bfloat16 or wider.
A program may use at most 768 MiB of HBM per device.

v0:
```python
import jax
import jax.numpy as jnp
from jax import lax
from jax.sharding import PartitionSpec as P


def solution(mesh):
    n_seq = mesh.shape["sp"]
    to_right = [(sender, sender + 1) for sender in range(n_seq - 1)]
    to_left = [(sender + 1, sender) for sender in range(n_seq - 1)]

    def local_layer(tokens, glob_pos, rel_bias, w_query, w_key, w_value, w_query_glob, w_out, w_up, w_down):
        local_rows = tokens.shape[0]
        local_heads = rel_bias.shape[0]
        window = (rel_bias.shape[1] - 1) // 2
        local_dim = w_query.shape[1]
        head_dim = local_dim // local_heads
        num_glob = glob_pos.shape[0]
        n_blocks = local_rows // window
        seq_len = local_rows * n_seq
        score_scale = head_dim ** -0.5
        row_start = lax.axis_index("sp") * local_rows
        heads_shape = (local_rows, local_heads, head_dim)
        glob_shape = (num_glob, local_heads, head_dim)

        def project(weight):
            return jnp.dot(tokens, weight, preferred_element_type=jnp.float32).astype(jnp.bfloat16)

        q_flat = project(w_query)
        k_flat = project(w_key)
        v_flat = project(w_value)
        local_slot = glob_pos - row_start
        is_owned = (local_slot >= 0) & (local_slot < local_rows)
        safe_slot = jnp.clip(local_slot, 0, local_rows - 1)
        zero_half = jnp.zeros((), jnp.bfloat16)

        def pick_rows(source):
            return jnp.where(is_owned[:, None], jnp.take(source, safe_slot, axis=0), zero_half)

        qg_part = jnp.dot(pick_rows(tokens), w_query_glob, preferred_element_type=jnp.float32).astype(jnp.bfloat16)
        glob_rows = lax.psum(jnp.stack([qg_part, pick_rows(k_flat), pick_rows(v_flat)]), "sp")
        glob_q = glob_rows[0].reshape(glob_shape)
        glob_k = glob_rows[1].reshape(glob_shape)
        glob_v = glob_rows[2].reshape(glob_shape)

        kv_loc = jnp.stack([k_flat, v_flat]).reshape((2,) + heads_shape)
        left_halo = lax.ppermute(kv_loc[:, local_rows - window:], "sp", to_right)
        right_halo = lax.ppermute(kv_loc[:, :window], "sp", to_left)
        kv_ext = jnp.concatenate([left_halo, kv_loc, right_halo], axis=1)
        kv_blocks = kv_ext.reshape(2, n_blocks + 2, window, local_heads, head_dim)
        kv_win = jnp.concatenate([kv_blocks[:, :-2], kv_blocks[:, 1:-1], kv_blocks[:, 2:]], axis=2)
        q_blocks = q_flat.reshape(n_blocks, window, local_heads, head_dim)

        rel_offs = jnp.arange(3 * window)[None, :] - jnp.arange(window)[:, None]
        in_band = (rel_offs >= 0) & (rel_offs <= 2 * window)
        band_bias = jnp.take(rel_bias, jnp.clip(rel_offs, 0, 2 * window), axis=1)
        blk_start = row_start + jnp.arange(n_blocks) * window
        key_pos = blk_start[:, None] - window + jnp.arange(3 * window)[None, :]
        key_ok = (key_pos >= 0) & (key_pos < seq_len)
        win_mask = in_band[None, None] & key_ok[:, None, None, :]
        win_scores = jnp.einsum("cqhd,ckhd->chqk", q_blocks, kv_win[0], preferred_element_type=jnp.float32)
        win_scores = jnp.where(win_mask, win_scores * score_scale + band_bias, -jnp.inf)
        query_pos = blk_start[:, None] + jnp.arange(window)[None, :]
        far_mask = jnp.abs(query_pos[:, :, None] - glob_pos[None, None, :]) > window
        glob_scores = jnp.einsum("cqhd,ghd->chqg", q_blocks, glob_k, preferred_element_type=jnp.float32)
        glob_scores = jnp.where(far_mask[:, None], glob_scores * score_scale, -jnp.inf)
        row_max = jnp.maximum(win_scores.max(axis=-1), glob_scores.max(axis=-1))[..., None]
        win_exp = jnp.exp(win_scores - row_max)
        glob_exp = jnp.exp(glob_scores - row_max)
        soft_sum = win_exp.sum(axis=-1, keepdims=True) + glob_exp.sum(axis=-1, keepdims=True)
        win_out = jnp.einsum("chqk,ckhd->cqhd", (win_exp / soft_sum).astype(jnp.bfloat16), kv_win[1], preferred_element_type=jnp.float32)
        win_out = win_out + jnp.einsum("chqg,ghd->cqhd", (glob_exp / soft_sum).astype(jnp.bfloat16), glob_v, preferred_element_type=jnp.float32)
        win_out = win_out.astype(jnp.bfloat16).reshape(heads_shape)

        part_scores = jnp.einsum("ghd,rhd->hgr", glob_q, kv_loc[0], preferred_element_type=jnp.float32) * score_scale
        part_max = part_scores.max(axis=-1)
        part_exp = jnp.exp(part_scores - part_max[..., None])
        part_sum = part_exp.sum(axis=-1)
        part_out = jnp.einsum("hgr,rhd->ghd", part_exp.astype(jnp.bfloat16), kv_loc[1], preferred_element_type=jnp.float32)
        glob_max = lax.pmax(part_max, "sp")
        rescale = jnp.exp(part_max - glob_max)
        tot_sum, tot_out = lax.psum((part_sum * rescale, part_out * rescale.T[:, :, None]), "sp")
        glob_out = (tot_out / tot_sum.T[:, :, None]).astype(jnp.bfloat16)
        slot_rows = jnp.where(is_owned, local_slot, local_rows)
        heads_out = win_out.at[slot_rows].set(glob_out, mode="drop")

        attn_part = jnp.dot(heads_out.reshape(local_rows, local_dim), w_out, preferred_element_type=jnp.float32)
        attn_proj = lax.psum(attn_part, "tp")
        hidden = (tokens.astype(jnp.float32) + attn_proj).astype(jnp.bfloat16)
        act_vals = jax.nn.gelu(jnp.dot(hidden, w_up, preferred_element_type=jnp.float32)).astype(jnp.bfloat16)
        mlp_out = lax.psum(jnp.dot(act_vals, w_down, preferred_element_type=jnp.float32), "tp")
        return (hidden.astype(jnp.float32) + mlp_out).astype(jnp.bfloat16)

    row_spec = P(("batch", "sp"), None)
    col_spec = P(None, "tp")
    head_spec = P("tp", None)
    in_specs = (row_spec, P("batch"), head_spec, col_spec, col_spec, col_spec, col_spec, head_spec, col_spec, head_spec)
    return jax.shard_map(local_layer, mesh=mesh, in_specs=in_specs, out_specs=row_spec, check_vma=False)
```

profile of v0, /device:TPU:97, one launch (start us, length us, event | category | flops | bytes accessed | tf_op | source)
XLA Modules:
  0.0 1989.8 jit_solution(8955865302713340951)
XLA Ops:
  6.6 11.9 convolution_convert_fusion.1
  18.5 4.4 copy.109
  22.9 11.8 convolution_convert_fusion.2
  34.7 4.4 copy.108
  39.1 2.5 pad_maximum_fusion.4
  41.6 4.0 collective-permute-start.1
  45.6 3.1 collective-permute-start
  48.7 4.4 copy.117
  53.1 4.4 copy.118
  57.5 11.5 gather_fusion.1
  69.0 4.9 gather_fusion.2
  73.8 4.9 gather_fusion.3
  80.3 5.0 fusion.50
  92.4 13.0 convolution_convert_fusion
  105.5 2.2 abs_compare_fusion
  111.2 709.0 %gather_fusion = f32[196608,5]{1,0:T(8,128)} fusion(f32[5,513]{0,1:T(8,128)S(1)} %copy.115, s32[196608]{0:T(1024)} %broadcast_clamp_fusion), kind=kCustom, calls=%fused_computation.2 | custom fusion | bytes 8650752 | tf_op jit(solution)/shard_map/jit(_take)/gather | solution.py:56
  820.2 56.2 %copy.116 = f32[256,768,5]{1,0,2:T(8,128)} copy(f32[256,768,5]{2,1,0:T(8,128)} %bitcast.5) | data formatting | bytes 7864320 | tf_op jit(solution)/shard_map/jit(_take)/gather | solution.py:56
  876.5 4.5 copy.113
  881.0 4.3 copy.151
  885.9 4.5 select_bitcast_fusion
  890.4 4.2 pad_maximum_fusion.1
  894.6 3.7 fusion.76
  899.8 6.5 fusion.75
  906.3 21.3 %fusion.9 = (f32[8,5,256]{2,1,0:T(8,128)S(1)}, f32[8,5,256,768]{3,2,1,0:T(8,128)}) fusion(f32[5,256,768]{2,1,0:T(8,128)} %select_bitcast_fusion, pred[8,256,768]{2,1,0:T(8,128)(4,1)} %broadcast_and_fusion, bf16[1,8,768,5,128]{4,2,1,3,0:T(8,128)(2,1)} %get-tuple-element.9, bf16[8,256,5,128]{1,0,3,2:T(8,128)(2,1)} %bitcast.87), kind=kOutput, calls=%fused_computation.24 | convolution fusion | flops 2044712960 | bytes 47489024 | tf_op jit(solution)/shard_map/cqhd,ckhd->chqk/dot_general | solution.py:61
  927.6 2.8 fusion.77
  930.4 2.2 copy.119
  932.6 13.4 fusion.13
  946.0 10.7 fusion.10
  956.7 15.3 fusion
  972.7 2.2 copy.127
  977.1 12.0 multiply_reduce_fusion
  989.0 22.1 %pmax.7 = f32[5,512]{1,0:T(8,128)S(1)} all-reduce(f32[5,512]{1,0:T(8,128)S(1)} %get-tuple-element.27), channel_id=1, replica_groups=mesh['batch'=1,'tp'=4,'sp'=8] {'sp'}, use_global_device_ids=true, to_apply=%region_6.8 | all-reduce | flops 2560 | bytes 20480 | tf_op jit(solution)/shard_map/pmax | solution.py:80
  1011.1 9.5 fusion.11
  1021.2 10.1 fusion.42
  1031.5 20.7 %fusion.14 = f32[8,5,128,256]{3,2,1,0:T(8,128)} fusion(f32[8,5,256,768]{3,2,1,0:T(8,128)} %get-tuple-element.26, f32[8,5,256]{2,1,0:T(8,128)} %copy.125, f32[8,5,256]{2,1,0:T(8,128)S(1)} %copy.123, f32[5,256,768]{2,1,0:T(8,128)} %select_bitcast_fusion, pred[8,256,768]{2,1,0:T(8,128)(4,1)} %broadcast_and_fusion, ...), kind=kOutput, calls=%fused_computation.31 | convolution fusion | flops 2060451840 | bytes 50151424 | tf_op jit(solution)/shard_map/chqk,ckhd->cqhd/dot_general | solution.py:71
  1052.3 13.0 fusion.28
  1065.3 6.2 copy.144
  1071.5 23.9 %psum.37 = f32[512,5]{0,1:T(8,128)S(1)} all-reduce(f32[512,5]{0,1:T(8,128)S(1)} %copy-done.11), channel_id=1, replica_groups=mesh['batch'=1,'tp'=4,'sp'=8] {'sp'}, use_global_device_ids=true, to_apply=%region_9.11 | all-reduce | flops 2560 | bytes 20480 | tf_op jit(solution)/shard_map/psum | solution.py:82
  1095.4 2.3 divide_convert_fusion.3
  1097.7 2.3 copy.134
  1100.0 46.6 %scatter_fusion = bf16[2048,5,128]{2,1,0:T(8,128)(2,1)} fusion(bf16[2048,5,128]{2,1,0:T(8,128)(2,1)} %bitcast.86, s32[512]{0:T(512)S(1)} %copy-done.13, bf16[512,5,128]{2,1,0:T(8,128)(2,1)} %copy.134), kind=kCustom, calls=%fused_computation.4 | custom fusion | bytes 1968128 | tf_op jit(solution)/shard_map/scatter | solution.py:85
  1146.7 6.1 copy.135
  1152.8 14.3 fusion.78
  1167.2 360.8 %all-reduce.9.cloned.1.call-done = f32[2048,2560]{1,0:T(8,128)} async-done(((f32[2048,2560]{1,0:T(8,128)}), f32[2048,2560]{1,0:T(8,128)}) %all-reduce.9.cloned.1.call-update) | async-done | bytes 20971536 | tf_op jit(solution)/shard_map/psum | solution.py:88
  1528.0 37.2 %fusion.74 = f32[2048,2560]{1,0:T(8,128)} fusion(bf16[2560,2560]{1,0:T(8,128)(2,1)} %param.20, f32[2048,2560]{1,0:T(8,128)} %all-reduce.9.cloned.1.call-done, bf16[2048,2560]{1,0:T(8,128)(2,1)} %param.12), kind=kOutput, calls=%fused_computation.112 | convolution fusion | flops 26859274240 | bytes 65536000 | tf_op jit(solution)/shard_map/dot_general | solution.py:90
  1565.2 37.5 %fusion.17 = f32[2048,2560]{1,0:T(8,128)} fusion(bf16[2560,2560]{1,0:T(8,128)(2,1)} %param.21, f32[2048,2560]{1,0:T(8,128)} %fusion.74), kind=kOutput, calls=%fused_computation.33 | convolution fusion | flops 26890731520 | bytes 55050240 | tf_op jit(solution)/shard_map/dot_general | solution.py:91
  1602.8 358.1 %all-reduce.11.cloned.1.call-done = f32[2048,2560]{1,0:T(8,128)} async-done(((f32[2048,2560]{1,0:T(8,128)}), f32[2048,2560]{1,0:T(8,128)}) %all-reduce.11.cloned.1.call-update) | async-done | bytes 20971536 | tf_op jit(solution)/shard_map/psum | solution.py:91
  1960.8 22.2 %add_convert_fusion = bf16[2048,2560]{1,0:T(8,128)(2,1)} fusion(f32[2048,2560]{1,0:T(8,128)} %all-reduce.11.cloned.1.call-done, f32[2048,2560]{1,0:T(8,128)} %all-reduce.9.cloned.1.call-done, bf16[2048,2560]{1,0:T(8,128)(2,1)} %param.12), kind=kLoop, calls=%fused_computation.19 | loop fusion | flops 31457280 | bytes 62914560 | tf_op jit(solution)/shard_map/convert_element_type | solution.py:92
  (62 shorter events, 18.2 us)
Async XLA Ops:
  6.5 1146.2 %copy-start = (bf16[640,2560]{1,0:T(8,128)(2,1)S(1)}, bf16[640,2560]{1,0:T(8,128)(2,1)}, u32[]{:S(2)}) copy-start(bf16[640,2560]{1,0:T(8,128)(2,1)} %param.19) | copy-start | bytes 9830404
  6.6 921.0 %all-reduce.5.cloned.1.call-start = ((), (), s32[]{:S(2)}) async-start(), calls=%async_computation | async-start | bytes 3932160 | tf_op jit(solution)/shard_map/psum | solution.py:41
  34.7 22.8 %copy-start.12 = (s32[512]{0:T(512)S(1)}, s32[512]{0:T(512)}, u32[]{:S(2)}) copy-start(s32[512]{0:T(512)} %param.13) | copy-start | bytes 6148
  41.6 848.8 %collective-permute-start.1 = (bf16[2,256,5,128]{3,1,2,0:T(8,128)(2,1)}, bf16[2,256,5,128]{3,1,2,0:T(8,128)(2,1)}, u32[]{:S(2)}, u32[]{:S(2)}) collective-permute-start(bf16[2,256,5,128]{3,1,2,0:T(8,128)(2,1)} %get-tuple-element.14), channel_id=1, source_target_pairs={{1,0},{2,1},{3,2},{4,3},{5,4},{6,5},{7,6},{9,8},{10,9},{11,10},{12... | collective-permute-start | bytes 1966088 | tf_op jit(solution)/shard_map/ppermute | solution.py:48
  45.6 844.9 %collective-permute-start = (bf16[2,256,5,128]{3,1,2,0:T(8,128)(2,1)}, bf16[2,256,5,128]{3,1,2,0:T(8,128)(2,1)}, u32[]{:S(2)}, u32[]{:S(2)}) collective-permute-start(bf16[2,256,5,128]{3,1,2,0:T(8,128)(2,1)} %get-tuple-element.13), channel_id=1, source_target_pairs={{0,1},{1,2},{2,3},{3,4},{4,5},{5,6},{6,7},{8,9},{9,10},{10,11},{11... | collective-permute-start | bytes 1966088 | tf_op jit(solution)/shard_map/ppermute | solution.py:47
  86.9 1008.5 %all-reduce.7.cloned.1.call-start = ((), (), s32[]{:S(2)}) async-start(), calls=%async_computation.1 | async-start | bytes 2621440 | tf_op jit(solution)/shard_map/psum | solution.py:82
  876.5 9.5 copy-start.9
  881.0 9.4 copy-start.4
  881.0 9.4 copy-start.5
  932.6 13.4 copy-start.7
  946.0 10.7 copy-start.2
  946.0 10.7 copy-start.6
  1011.1 10.1 copy-start.3
  1031.4 496.6 %all-reduce.9.cloned.1.call-start = ((), (), s32[]{:S(2)}) async-start(), calls=%async_computation.2 | async-start | bytes 41943040 | tf_op jit(solution)/shard_map/psum | solution.py:88
  1031.5 20.8 %copy-start.8 = (pred[8,256,512]{1,2,0:T(8,128)(4,1)S(1)}, pred[8,256,512]{1,2,0:T(8,128)(4,1)}, u32[]{:S(2)}) copy-start(pred[8,256,512]{1,2,0:T(8,128)(4,1)} %abs_compare_fusion) | copy-start | bytes 3145732
  1031.5 20.8 %copy-start.10 = (bf16[1,512,640]{1,2,0:T(8,128)(2,1)S(1)}, bf16[1,512,640]{1,2,0:T(8,128)(2,1)}, u32[]{:S(2)}) copy-start(bf16[1,512,640]{1,2,0:T(8,128)(2,1)} %copy.127) | copy-start | bytes 1966084
  1052.3 19.2 copy-start.11
  1065.3 34.7 %copy-start.13 = (s32[512]{0:T(512)S(1)}, s32[512]{0:T(512)}, u32[]{:S(2)}) copy-start(s32[512]{0:T(512)} %compare_select_fusion.2) | copy-start | bytes 6148
  1167.1 793.7 %all-reduce.11.cloned.1.call-start = ((), (), s32[]{:S(2)}) async-start(), calls=%async_computation.3 | async-start | bytes 41943040 | tf_op jit(solution)/shard_map/psum | solution.py:91
  1960.8 22.2 %copy-start.1 = (bf16[640,2560]{1,0:T(8,128)(2,1)S(1)}, bf16[640,2560]{1,0:T(8,128)(2,1)}, u32[]{:S(2)}) copy-start(bf16[640,2560]{1,0:T(8,128)(2,1)} %param.19) | copy-start | bytes 9830404
Sparse Core Ops, SparseCore 0:
  87.0 60.6 all-reduce.4
  1031.5 59.4 all-reduce.6
  1167.3 360.6 all-reduce.8
  1602.9 357.8 all-reduce.10
where the time goes:
time: 2020 us; the launch traced here: 1990 us
  local copies, waits for them, and re-layouts  897 us (44%)
  waiting for transfers between devices  719 us (36%)
  matrix products  221 us (11%)
  other arithmetic  85.1 us (4%)
  blocking collectives  46 us (2%)
    gather x2, local copies, waits for them, and re-layouts, local_layer(): band_bias = jnp.take(rel_bias, jnp.clip(rel_offs, 0, 2 * window), axis=1)  765 us
    psum x1, waiting for transfers between devices, local_layer(): attn_proj = lax.psum(attn_part, 'tp')  361 us
    psum x1, waiting for transfers between devices, local_layer(): lax.psum(jnp.dot(act_vals, w_down, preferred_element_type=jnp.float32), '...  358 us
    scatter x2, local copies, waits for them, and re-layouts, local_layer(): heads_out = win_out.at[slot_rows].set(glob_out, mode='drop')  52.7 us
  transfers between devices with their start and end apart: 6, of which 2 were waited for; matrix products, arithmetic and copies ran while one was open for 46% of the time, Pallas kernels for 0%

commit v1 on v0

v1 whole, which is shorter than its diff:
```python
import functools
import math

import jax
import jax.numpy as jnp
from jax import lax
from jax.experimental import pallas as pl
from jax.experimental.pallas import tpu as pltpu
from jax.sharding import PartitionSpec as P

LOG2E = math.log2(math.e)
NEG_INF = float("-inf")
F32 = jnp.float32
BF16 = jnp.bfloat16


def _dot(lhs, rhs):
    return jnp.dot(lhs, rhs, preferred_element_type=F32)


def _dot_t(lhs, rhs):
    return lax.dot_general(lhs, rhs, (((1,), (1,)), ((), ())), preferred_element_type=F32)


def _qkv_kernel(x_ref, wq_ref, wk_ref, wv_ref, q_ref, k_ref, v_ref):
    x = x_ref[...]
    q_ref[...] = _dot(x, wq_ref[...]).astype(BF16)
    k_ref[...] = _dot(x, wk_ref[...]).astype(BF16)
    v_ref[...] = _dot(x, wv_ref[...]).astype(BF16)


def _project_qkv(tokens, w_query, w_key, w_value):
    rows, depth = tokens.shape
    cols = w_query.shape[1]
    blk = rows // 4
    w_spec = pl.BlockSpec((depth, cols), lambda i: (0, 0), pipeline_mode=pl.Buffered(1))
    o_spec = pl.BlockSpec((blk, cols), lambda i: (i, 0))
    return pl.pallas_call(
        _qkv_kernel,
        grid=(rows // blk,),
        in_specs=[pl.BlockSpec((blk, depth), lambda i: (i, 0)), w_spec, w_spec, w_spec],
        out_specs=[o_spec] * 3,
        out_shape=[jax.ShapeDtypeStruct((rows, cols), BF16)] * 3,
        cost_estimate=pl.CostEstimate(
            flops=6 * rows * depth * cols,
            bytes_accessed=2 * (rows * depth + 3 * depth * cols + 3 * rows * cols),
            transcendentals=0,
        ),
        name="qkv_proj",
    )(tokens, w_query, w_key, w_value)


def _glob_kernel(scale, q_ref, k_ref, v_ref, o_ref, m_ref, l_ref):
    scores = _dot_t(q_ref[...], k_ref[...]) * scale
    top = jnp.max(scores, axis=1, keepdims=True)
    probs = jnp.exp2(scores - top)
    total = jnp.sum(probs, axis=1, keepdims=True)
    o_ref[...] = _dot(probs.astype(BF16), v_ref[...])
    m_ref[...] = jnp.broadcast_to(top, m_ref.shape)
    l_ref[...] = jnp.broadcast_to(total, l_ref.shape)


def _glob_partial(glob_q, keys, values, n_heads, scale):
    n_glob, width = glob_q.shape
    rows = keys.shape[0]
    hd = width // n_heads
    blk = n_glob // 2
    q_spec = pl.BlockSpec((blk, hd), lambda h, i: (i, h))
    kv_spec = pl.BlockSpec((rows, hd), lambda h, i: (0, h))
    return pl.pallas_call(
        functools.partial(_glob_kernel, scale * LOG2E),
        grid=(n_heads, n_glob // blk),
        in_specs=[q_spec, kv_spec, kv_spec],
        out_specs=[q_spec] * 3,
        out_shape=[jax.ShapeDtypeStruct((n_glob, width), F32)] * 3,
        cost_estimate=pl.CostEstimate(
            flops=16 * n_glob * rows * width,
            bytes_accessed=4 * rows * width + 14 * n_glob * width,
            transcendentals=n_glob * rows * n_heads,
        ),
        name="glob_attn",
    )(glob_q, keys, values)


def _local_kernel(window, seq_len, scale, start_ref, q_ref, k_ref, v_ref, gk_ref, gv_ref, rb_ref, gpos_ref, o_ref, bias_ref):
    blk = pl.program_id(1)
    span = 3 * window

    @pl.when(blk == 0)
    def _():
        bias = jnp.broadcast_to(rb_ref[0], (window, span))
        row = lax.broadcasted_iota(jnp.int32, (window, span), 0)
        for bit in range(window.bit_length() - 1):
            bias = jnp.where(((row >> bit) & 1) == 1, pltpu.roll(bias, 1 << bit, 1), bias)
        bias_ref[...] = bias

    first = start_ref[0] + blk * window
    key_pos = first - window + lax.broadcasted_iota(jnp.int32, (1, span), 1)
    edge = jnp.where((key_pos >= 0) & (key_pos < seq_len), 0.0, NEG_INF).astype(F32)
    q = q_ref[...]
    rows = pl.ds(pl.multiple_of(blk * window, window), span)
    win = _dot_t(q, k_ref[rows, :]) * scale + (bias_ref[...] + edge)
    dist = first + lax.broadcasted_iota(jnp.int32, (window, 1), 0) - gpos_ref[...]
    glob = _dot_t(q, gk_ref[...]) * scale
    glob = jnp.where(jnp.abs(dist) > window, glob, NEG_INF)
    top = jnp.maximum(jnp.max(win, axis=1, keepdims=True), jnp.max(glob, axis=1, keepdims=True))
    win = jnp.exp2(win - top)
    glob = jnp.exp2(glob - top)
    inv = 1.0 / (jnp.sum(win, axis=1, keepdims=True) + jnp.sum(glob, axis=1, keepdims=True))
    out = _dot((win * inv).astype(BF16), v_ref[rows, :])
    out = out + _dot((glob * inv).astype(BF16), gv_ref[...])
    o_ref[...] = out.astype(BF16)


def _local_attn(row_start, q, k_ext, v_ext, glob_k, glob_v, rel_bias, glob_pos, window, seq_len, scale):
    rows, width = q.shape
    n_heads = rel_bias.shape[0]
    hd = width // n_heads
    n_glob = glob_k.shape[0]
    span = 3 * window
    pad = jnp.full((n_heads, span - rel_bias.shape[1]), NEG_INF, F32)
    bias_rows = jnp.concatenate([rel_bias * LOG2E, pad], axis=1)[:, None, :]
    q_spec = pl.BlockSpec((window, hd), lambda h, c, s: (c, h))
    kv_spec = pl.BlockSpec((k_ext.shape[0], hd), lambda h, c, s: (0, h))
    g_spec = pl.BlockSpec((n_glob, hd), lambda h, c, s: (0, h))
    grid_spec = pltpu.PrefetchScalarGridSpec(
        num_scalar_prefetch=1,
        grid=(n_heads, rows // window),
        in_specs=[
            q_spec,
            kv_spec,
            kv_spec,
            g_spec,
            g_spec,
            pl.BlockSpec((1, 1, span), lambda h, c, s: (h, 0, 0)),
            pl.BlockSpec((1, n_glob), lambda h, c, s: (0, 0)),
        ],
        out_specs=q_spec,
        scratch_shapes=[pltpu.VMEM((window, span), F32)],
    )
    return pl.pallas_call(
        functools.partial(_local_kernel, window, seq_len, scale * LOG2E),
        grid_spec=grid_spec,
        out_shape=jax.ShapeDtypeStruct((rows, width), BF16),
        cost_estimate=pl.CostEstimate(
            flops=16 * rows * (span + n_glob) * width,
            bytes_accessed=2 * (2 * rows * width + 2 * (k_ext.shape[0] + n_glob) * width),
            transcendentals=n_heads * rows * (span + n_glob),
        ),
        name="local_attn",
    )(row_start[None], q, k_ext, v_ext, glob_k, glob_v, bias_rows, glob_pos[None, :])


def solution(mesh):
    n_seq = mesh.shape["sp"]
    n_tp = mesh.shape["tp"]
    to_right = [(sender, sender + 1) for sender in range(n_seq - 1)]
    to_left = [(sender + 1, sender) for sender in range(n_seq - 1)]
    n_row_chunks = 2
    n_hid_chunks = 2

    def local_layer(tokens, glob_pos, rel_bias, w_query, w_key, w_value, w_query_glob, w_out, w_up, w_down):
        local_rows, model_dim = tokens.shape
        n_heads, rel_width = rel_bias.shape
        window = (rel_width - 1) // 2
        width = w_query.shape[1]
        hd = width // n_heads
        n_glob = glob_pos.shape[0]
        seq_len = local_rows * n_seq
        scale = hd ** -0.5
        sp_index = lax.axis_index("sp")
        tp_index = lax.axis_index("tp")
        row_start = (sp_index * local_rows).astype(jnp.int32)

        def share(shard):
            part = shard.shape[0] // n_seq
            piece = lax.dynamic_slice_in_dim(shard, sp_index * part, part, 0)
            return lax.all_gather(piece, ("tp", "sp"), axis=0, tiled=True)

        hid = w_up.shape[1] // n_hid_chunks
        out_full = share(w_out)
        up_full, down_full = [], []
        for j in range(n_hid_chunks):
            up_full.append(share(w_up[:, j * hid:(j + 1) * hid]).reshape(n_tp, model_dim, hid))
            down_full.append(share(w_down[j * hid:(j + 1) * hid]))

        q, k, v = _project_qkv(tokens, w_query, w_key, w_value)

        edges = jnp.stack([k, v])
        left = lax.ppermute(edges[:, local_rows - window:], "sp", to_right)
        right = lax.ppermute(edges[:, :window], "sp", to_left)
        k_ext = jnp.concatenate([left[0], k, right[0]], axis=0)
        v_ext = jnp.concatenate([left[1], v, right[1]], axis=0)

        slot = glob_pos - row_start
        pick = (slot[:, None] == jnp.arange(local_rows, dtype=jnp.int32)[None, :]).astype(BF16)
        qg_rows = _dot(_dot(pick, tokens).astype(BF16), w_query_glob).astype(BF16)
        mine = jnp.concatenate([qg_rows, _dot(pick, k).astype(BF16), _dot(pick, v).astype(BF16)], axis=1)
        mine = lax.all_to_all(mine, "sp", 0, 0, tiled=True)
        mine = mine.reshape(n_seq, n_glob // n_seq, 3 * width)
        mine = mine.astype(F32).sum(axis=0).astype(BF16)
        glob_q = lax.all_gather(mine[:, :width], "sp", axis=0, tiled=True)
        glob_k = lax.all_gather(mine[:, width:2 * width], "sp", axis=0, tiled=True)
        glob_v = lax.all_gather(mine[:, 2 * width:], "sp", axis=0, tiled=True)

        part_out, part_max, part_sum = _glob_partial(glob_q, k, v, n_heads, scale)
        parts = jnp.concatenate([part_out, part_max[:, ::hd], part_sum[:, ::hd]], axis=1)
        parts = lax.all_to_all(parts, "sp", 0, 0, tiled=True)
        parts = parts.reshape(n_seq, n_glob // n_seq, width + 2 * n_heads)
        part_max = parts[:, :, width:width + n_heads]
        factor = jnp.exp2(part_max - part_max.max(axis=0))
        tot_sum = (parts[:, :, width + n_heads:] * factor).sum(axis=0)
        part_out = parts[:, :, :width].reshape(n_seq, n_glob // n_seq, n_heads, hd)
        tot_out = (part_out * factor[..., None]).sum(axis=0) / tot_sum[..., None]
        glob_out = tot_out.astype(BF16).reshape(n_glob // n_seq, width)
        glob_out = lax.all_gather(glob_out, "sp", axis=0, tiled=True)

        win_out = _local_attn(row_start, q, k_ext, v_ext, glob_k, glob_v, rel_bias, glob_pos, window, seq_len, scale)

        put = jnp.arange(local_rows, dtype=jnp.int32)[:, None] == slot[None, :]
        is_glob = put.any(axis=1, keepdims=True)
        heads_out = jnp.where(is_glob, _dot(put.astype(BF16), glob_out).astype(BF16), win_out)

        blk = local_rows // (n_row_chunks * n_tp)
        heads_out = heads_out.reshape(n_row_chunks, n_tp, blk, width)
        heads_out = lax.all_to_all(heads_out, "tp", 1, 1, tiled=True)
        attn_rows = heads_out.transpose(0, 2, 1, 3).reshape(n_row_chunks * blk, n_tp * width)
        own_rows = lax.dynamic_index_in_dim(tokens.reshape(n_row_chunks, n_tp, blk, model_dim), tp_index, 1, keepdims=False)
        own_rows = own_rows.reshape(n_row_chunks * blk, model_dim)
        hidden = (own_rows.astype(F32) + _dot(attn_rows, out_full)).astype(BF16)

        acts = [
            jnp.concatenate([jax.nn.gelu(_dot(hidden, w)).astype(BF16) for w in up_full[j]], axis=1)
            for j in range(n_hid_chunks)
        ]
        acc = sum(_dot(acts[j], down_full[j]) for j in range(n_hid_chunks - 1))
        outs = []
        for i in range(n_row_chunks):
            rows = slice(i * blk, (i + 1) * blk)
            mlp = acc[rows] + _dot(acts[-1][rows], down_full[-1])
            out = (hidden[rows].astype(F32) + mlp).astype(BF16)
            outs.append(lax.all_gather(out, "tp", axis=0, tiled=True))
        return jnp.concatenate(outs, axis=0)

    row_spec = P(("batch", "sp"), None)
    col_spec = P(None, "tp")
    head_spec = P("tp", None)
    in_specs = (row_spec, P("batch"), head_spec, col_spec, col_spec, col_spec, col_spec, head_spec, col_spec, head_spec)
    return jax.shard_map(local_layer, mesh=mesh, in_specs=in_specs, out_specs=row_spec, check_vma=False)
```

time: 2020 us -> 645 us (0.32); the launches traced: 1990 us -> 640 us
  local copies, waits for them, and re-layouts: 897 us -> 49.3 us
  waiting for transfers between devices: 719 us -> 185 us
  Pallas kernels: 0 us -> 97.3 us
  matrix products: 221 us -> 127 us
  blocking collectives: 46 us -> 111 us
  other arithmetic: 85.1 us -> 30.8 us
    gather x5 -> x0, local copies, waits for them, and re-layouts: 786 us -> none  [the longest x2 765 us: local_layer(): band_bias = jnp.take(rel_bias, jnp.clip(rel_offs, 0, 2 * window), axis=1)]
    psum x4 -> x0, waiting for transfers between devices: 719 us -> none  [the longest x1 361 us: local_layer(): attn_proj = lax.psum(attn_part, 'tp')]
    all_gather x0 -> x4, blocking collectives: none -> 111 us  [the longest x1 41.1 us: local_layer(): glob_k = lax.all_gather(mine[:, width:2 * width], 'sp', axis=0, tiled=True)]
    pallas_call x0 -> x3, Pallas kernels: none -> 97.3 us  [the longest x1 52.7 us: _local_attn(): pl.pallas_call(functools.partial(_local_kernel, window, seq_len, scale *...]
    all_gather x0 -> x7, waiting for transfers between devices: none -> 97.3 us  [the longest x2 97.2 us: local_layer(): outs.append(lax.all_gather(out, 'tp', axis=0, tiled=True))]
    dot_general x13 -> x16, matrix products: 221 us -> 127 us  [_dot(): return jnp.dot(lhs, rhs, preferred_element_type=F32)]
    scatter x2 -> x0, local copies, waits for them, and re-layouts: 52.7 us -> none  [local_layer(): heads_out = win_out.at[slot_rows].set(glob_out, mode='drop')]
    ppermute x2, waiting for transfers between devices: 0.01 us -> 46 us  [the longest x1 45.1 us: local_layer(): left = lax.ppermute(edges[:, local_rows - window:], 'sp', to_right)]
  transfers between devices with their start and end apart: 6 -> 12, of which waited for: 2 -> 5; matrix products, arithmetic and copies ran while one was open for 46% -> 27% of each run, Pallas kernels for 0% -> 15%
where the time goes in v1:
time: 645 us; the launch traced here: 640 us
  waiting for transfers between devices  185 us (29%)
  matrix products  127 us (20%)
  blocking collectives  111 us (17%)
  Pallas kernels  97.3 us (15%)
  local copies, waits for them, and re-layouts  49.3 us (8%)
  other arithmetic  30.8 us (5%)
  starting transfers between devices  24.7 us (4%)
  between operations  14.3 us (2%)
    dot_general x16, matrix products, _dot(): return jnp.dot(lhs, rhs, preferred_element_type=F32)  127 us
    all_gather x2, waiting for transfers between devices, local_layer(): outs.append(lax.all_gather(out, 'tp', axis=0, tiled=True))  97.2 us
    pallas_call x1, Pallas kernels, _local_attn(): pl.pallas_call(functools.partial(_local_kernel, window, seq_len, scale *...  52.7 us
    ppermute x1, waiting for transfers between devices, local_layer(): left = lax.ppermute(edges[:, local_rows - window:], 'sp', to_right)  45.1 us
    all_gather x1, blocking collectives, local_layer(): glob_k = lax.all_gather(mine[:, width:2 * width], 'sp', axis=0, tiled=True)  41.1 us
    all_to_all x1, waiting for transfers between devices, local_layer(): heads_out = lax.all_to_all(heads_out, 'tp', 1, 1, tiled=True)  40.8 us
    pallas_call x1, Pallas kernels, _project_qkv(): pl.pallas_call(_qkv_kernel, grid=(rows // blk,), in_specs=[pl.BlockSpec((...  30.7 us
    all_gather x1, blocking collectives, local_layer(): glob_out = lax.all_gather(glob_out, 'sp', axis=0, tiled=True)  24.7 us
  transfers between devices with their start and end apart: 12, of which 5 were waited for; matrix products, arithmetic and copies ran while one was open for 27% of the time, Pallas kernels for 15%

profile of v1, /device:TPU:97, one launch (start us, length us, event | category | flops | bytes accessed | tf_op | source)
XLA Modules:
  0.0 639.5 jit_solution(18302850394070049624)
XLA Ops:
  6.6 1.9 constant_dynamic-slice_fusion.4
  8.6 8.3 %fusion.142 = (bf16[2560,1280]{1,0:T(8,128)(2,1)}, bf16[2560,1280]{1,0:T(8,128)(2,1)S(1)}) fusion(bf16[2560,2560]{1,0:T(8,128)(2,1)} %param.18), kind=kLoop, calls=%fused_computation.151 | loop fusion | bytes 26214400 | tf_op jit(solution)/shard_map/slice | solution.py:184
  18.0 2.1 constant_dynamic-slice_fusion.3
  20.3 8.3 %fusion.143 = (bf16[1280,2560]{1,0:T(8,128)(2,1)S(1)}, bf16[1280,2560]{1,0:T(8,128)(2,1)}) fusion(bf16[2560,2560]{1,0:T(8,128)(2,1)} %param.19), kind=kLoop, calls=%fused_computation.152 | loop fusion | bytes 26214400 | tf_op jit(solution)/shard_map/slice | solution.py:185
  29.6 2.1 constant_dynamic-slice_fusion
  31.8 30.7 %qkv_proj.1 = (bf16[2048,640]{1,0:T(8,128)(2,1)}, bf16[2048,640]{1,0:T(8,128)(2,1)}, bf16[2048,640]{1,0:T(8,128)(2,1)}) custom-call(bf16[2048,2560]{1,0:T(8,128)(2,1)} %x_ref.1, bf16[2560,640]{1,0:T(8,128)(2,1)} %wq_ref.1, bf16[2560,640]{1,0:T(8,128)(2,1)} %wk_ref.1, bf16[2560,640]{1,0:T(8,128)(2,1)} %wv_ref.1), custom_call_target="tpu_custom_call" | custom-call | flops 20132659200 | bytes 28180480 | tf_op jit(solution)/shard_map/qkv_proj/pallas_call | solution.py:38
  62.6 4.7 fusion.136
  67.3 2.8 fusion.137
  70.1 12.7 %convolution_convert_fusion.1 = bf16[512,640]{1,0:T(8,128)(2,1)} fusion(bf16[2560,640]{1,0:T(8,128)(2,1)S(1)} %copy-done, bf16[2048,2560]{1,0:T(8,128)(2,1)} %x_ref.1, s32[512]{0:T(512)S(1)} %broadcast_subtract_fusion), kind=kOutput, calls=%fused_computation.127 | convolution fusion | flops 7049117696 | bytes 14419968 | tf_op jit(solution)/shard_map/dot_general | solution.py:18
  82.8 2.9 pad_maximum_fusion.4
  85.7 6.5 %all-to-all-start = ((bf16[8,64,1920]{2,1,0:T(8,128)(2,1)}), bf16[8,64,1920]{2,1,0:T(8,128)(2,1)}, u32[]{:S(2)}, u32[]{:S(2)}) async-start(bf16[8,64,1920]{2,1,0:T(8,128)(2,1)} %bitcast.52), calls=%async_computation | async-start | bytes 3932160 | tf_op jit(solution)/shard_map/all_to_all | solution.py:199
  93.5 3.9 collective-permute-start
  97.3 2.2 collective-permute-start.1
  100.6 45.1 %collective-permute-done = bf16[2,256,640]{2,1,0:T(8,128)(2,1)S(1)} collective-permute-done((bf16[2,256,640]{2,1,0:T(8,128)(2,1)S(1)}, bf16[2,256,640]{2,1,0:T(8,128)(2,1)S(1)}, u32[]{:S(2)}, u32[]{:S(2)}) %collective-permute-start) | collective-permute-done | bytes 655392 | tf_op jit(solution)/shard_map/ppermute | solution.py:190
  146.8 7.3 %pad_maximum_fusion.2 = (bf16[2560,640]{1,0:T(8,128)(2,1)}, bf16[2560,640]{1,0:T(8,128)(2,1)}) fusion(bf16[256,640]{1,0:T(8,128)(2,1)S(1)} %get-tuple-element.28, bf16[2048,640]{1,0:T(8,128)(2,1)S(1)} %copy-done.2, bf16[256,640]{1,0:T(8,128)(2,1)S(1)} %get-tuple-element.26, bf16[256,640]{1,0:T(8,128)(2,1)S(1)} %get-tuple-element.27, ...), kind=kLoop, calls=%fused_computation.49 | loop fusion | flops 19660800 | bytes 13107200 | tf_op jit(solution)/shard_map/concatenate | solution.py:192
  156.0 20.7 %all_gather.33.q_ref = bf16[512,640]{1,0:T(8,128)(2,1)} all-gather(bf16[64,640]{1,0:T(8,128)(2,1)S(1)} %get-tuple-element.31), channel_id=1, replica_groups=mesh['batch'=1,'tp'=4,'sp'=8] {'sp'}, dimensions={0}, use_global_device_ids=true | all-gather | bytes 737280 | tf_op jit(solution)/shard_map/all_gather | solution.py:202
  176.7 13.8 %glob_attn.1 = (f32[512,640]{1,0:T(8,128)}, f32[512,640]{1,0:T(8,128)}, f32[512,640]{1,0:T(8,128)}) custom-call(bf16[512,640]{1,0:T(8,128)(2,1)} %all_gather.33.q_ref, bf16[2048,640]{1,0:T(8,128)(2,1)} %get-tuple-element.11.k_ref, bf16[2048,640]{1,0:T(8,128)(2,1)} %get-tuple-element.12.v_ref), custom_call_target="tpu_custom_call" | custom-call | flops 10737418240 | bytes 9830400 | tf_op jit(solution)/shard_map/glob_attn/pallas_call | solution.py:70
  190.6 2.4 slice.81
  193.0 2.4 slice.82
  195.5 2.6 pad_maximum_fusion.5
  198.1 7.7 %all-to-all-start.1 = ((f32[8,64,650]{2,1,0:T(8,128)}), f32[8,64,650]{2,1,0:T(8,128)S(1)}, u32[]{:S(2)}, u32[]{:S(2)}) async-start(f32[8,64,650]{2,1,0:T(8,128)} %bitcast.3), calls=%async_computation.1 | async-start | bytes 3145728 | tf_op jit(solution)/shard_map/all_to_all | solution.py:208
  205.8 41.1 %all_gather.35.gk_ref = bf16[512,640]{1,0:T(8,128)(2,1)} all-gather(bf16[64,640]{1,0:T(8,128)(2,1)S(1)} %get-tuple-element.30), channel_id=1, replica_groups=mesh['batch'=1,'tp'=4,'sp'=8] {'sp'}, dimensions={0}, use_global_device_ids=true | all-gather | bytes 737280 | tf_op jit(solution)/shard_map/all_gather | solution.py:203
  246.9 24.6 %all_gather.36.gv_ref = bf16[512,640]{1,0:T(8,128)(2,1)} all-gather(bf16[64,640]{1,0:T(8,128)(2,1)S(1)} %get-tuple-element.29), channel_id=1, replica_groups=mesh['batch'=1,'tp'=4,'sp'=8] {'sp'}, dimensions={0}, use_global_device_ids=true | all-gather | bytes 737280 | tf_op jit(solution)/shard_map/all_gather | solution.py:204
  271.6 52.7 %local_attn.1 = bf16[2048,640]{1,0:T(8,128)(2,1)} custom-call(s32[1]{0:T(128)} %bitcast.4.start_ref, bf16[2048,640]{1,0:T(8,128)(2,1)} %get-tuple-element.16.q_ref, bf16[2560,640]{1,0:T(8,128)(2,1)} %get-tuple-element.32.k_ref, bf16[2560,640]{1,0:T(8,128)(2,1)} %get-tuple-element.33.v_ref, bf16[512,640]{1,0:T(8,128)(2,1)} %all_gather.35.gk_ref, ...), custom_call_target="tpu_custom_call" | custom-call | flops 26843545600 | bytes 13107200 | tf_op jit(solution)/shard_map/local_attn/pallas_call | solution.py:141
  324.5 1.9 mul.131
  328.4 24.7 %all_gather.34 = bf16[512,640]{1,0:T(8,128)(2,1)S(1)} all-gather(bf16[64,640]{1,0:T(8,128)(2,1)S(1)} %fusion.140), channel_id=1, replica_groups=mesh['batch'=1,'tp'=4,'sp'=8] {'sp'}, dimensions={0}, use_global_device_ids=true | all-gather | bytes 737280 | tf_op jit(solution)/shard_map/all_gather | solution.py:216
  357.4 4.1 all-to-all-start.2
  361.4 3.4 constant_dynamic-slice_fusion.5
  364.8 40.8 %all-to-all-done.2 = bf16[2,4,256,640]{3,2,0,1:T(8,128)(2,1)S(1)} async-done(((bf16[2,4,256,640]{3,2,0,1:T(8,128)(2,1)}), bf16[2,4,256,640]{3,2,0,1:T(8,128)(2,1)S(1)}, u32[]{:S(2)}, u32[]{:S(2)}) %all-to-all-start.2) | async-done | bytes 2621472 | tf_op jit(solution)/shard_map/all_to_all | solution.py:226
  405.7 2.0 copy.19
  408.2 11.6 %fusion.24 = bf16[512,2560]{1,0:T(8,128)(2,1)} fusion(bf16[512,2560]{1,0:T(8,128)(2,1)} %bitcast.54, bf16[512,2560]{1,0:T(8,128)(2,1)S(1)} %bitcast.53, bf16[2560,2560]{1,0:T(8,128)(2,1)} %all-gather.8.cloned.1.call-done), kind=kOutput, calls=%fused_computation.27 | convolution fusion | flops 6714818560 | bytes 20971520 | tf_op jit(solution)/shard_map/dot_general | solution.py:18
  419.8 7.7 %fusion.103 = bf16[512,1280]{1,0:T(8,128)(2,1)S(1)} fusion(bf16[512,2560]{1,0:T(8,128)(2,1)} %fusion.24, bf16[10240,1280]{1,0:T(8,128)(2,1)} %all-gather.14.cloned.1.call-done), kind=kOutput, calls=%fused_computation.99 | convolution fusion | flops 3361341440 | bytes 10485760 | tf_op jit(solution)/shard_map/dot_general | solution.py:18
  427.5 3.4 copy-done.8
  431.6 3.9 fusion.115
  435.5 3.9 fusion.91
  439.4 3.9 fusion.127
  443.3 3.7 pad_maximum_fusion.1
  447.0 8.8 %fusion.43 = bf16[512,1280]{1,0:T(8,128)(2,1)} fusion(bf16[512,2560]{1,0:T(8,128)(2,1)} %fusion.24, bf16[10240,1280]{1,0:T(8,128)(2,1)} %all-gather.10.cloned.1.call-done), kind=kOutput, calls=%fused_computation.59 | convolution fusion | flops 3361341440 | bytes 10485760 | tf_op jit(solution)/shard_map/dot_general | solution.py:18
  455.9 3.5 copy-done.9
  459.4 4.9 fusion.55
  464.3 5.0 fusion.67
  469.3 5.0 fusion.79
  474.3 21.8 %fusion.16 = f32[512,2560]{1,0:T(8,128)} fusion(bf16[5120,2560]{1,0:T(8,128)(2,1)} %all-gather.12.cloned.1.call-done, bf16[512,1280]{1,0:T(8,128)(2,1)} %fusion.79, bf16[512,1280]{1,0:T(8,128)(2,1)} %fusion.67, bf16[512,1280]{1,0:T(8,128)(2,1)} %fusion.55, bf16[512,1280]{1,0:T(8,128)(2,1)} %fusion.43), kind=kOutput, calls=%fused_computation.17 | convolution fusion | flops 13442744320 | bytes 36700160 | tf_op jit(solution)/shard_map/dot_general | solution.py:18
  496.1 14.5 %fusion.31 = bf16[256,2560]{1,0:T(8,128)(2,1)} fusion(bf16[5120,2560]{1,0:T(8,128)(2,1)} %all-gather.16.cloned.1.call-done, bf16[512,5120]{1,0:T(8,128)(2,1)} %pad_maximum_fusion.1, f32[512,2560]{1,0:T(8,128)} %fusion.16, bf16[512,2560]{1,0:T(8,128)(2,1)S(1)} %copy-done.11), kind=kOutput, calls=%fused_computation.47 | convolution fusion | flops 6713507840 | bytes 34078720 | tf_op jit(solution)/shard_map/dot_general | solution.py:18
  510.7 14.4 %fusion.32 = bf16[256,2560]{1,0:T(8,128)(2,1)} fusion(bf16[5120,2560]{1,0:T(8,128)(2,1)} %all-gather.16.cloned.1.call-done, bf16[512,5120]{1,0:T(8,128)(2,1)} %pad_maximum_fusion.1, f32[512,2560]{1,0:T(8,128)} %fusion.16, bf16[512,2560]{1,0:T(8,128)(2,1)S(1)} %copy-done.11), kind=kOutput, calls=%fused_computation.48 | convolution fusion | flops 6713507840 | bytes 34078720 | tf_op jit(solution)/shard_map/dot_general | solution.py:18
  525.2 40.7 %all-gather.18.cloned.1.call-done = bf16[1024,2560]{1,0:T(8,128)(2,1)} async-done(((bf16[256,2560]{1,0:T(8,128)(2,1)}), bf16[1024,2560]{1,0:T(8,128)(2,1)}) %all-gather.18.cloned.1.call-update) | async-done | bytes 5242896 | tf_op jit(solution)/shard_map/all_gather | solution.py:242
  565.9 56.5 %all-gather.20.cloned.1.call-done = bf16[1024,2560]{1,0:T(8,128)(2,1)} async-done(((bf16[256,2560]{1,0:T(8,128)(2,1)}), bf16[1024,2560]{1,0:T(8,128)(2,1)}) %all-gather.20.cloned.1.call-update) | async-done | bytes 5242896 | tf_op jit(solution)/shard_map/all_gather | solution.py:242
  622.4 9.8 %pad_maximum_fusion = bf16[2048,2560]{1,0:T(8,128)(2,1)} fusion(bf16[1024,2560]{1,0:T(8,128)(2,1)} %all-gather.20.cloned.1.call-done, bf16[1024,2560]{1,0:T(8,128)(2,1)} %all-gather.18.cloned.1.call-done), kind=kLoop, calls=%fused_computation | loop fusion | flops 20971520 | bytes 20971520 | tf_op jit(solution)/shard_map/concatenate | solution.py:243
  (66 shorter events, 15.5 us)
Async XLA Ops:
  6.5 63.6 %copy-start = (bf16[2560,640]{1,0:T(8,128)(2,1)S(1)}, bf16[2560,640]{1,0:T(8,128)(2,1)}, u32[]{:S(2)}) copy-start(bf16[2560,640]{1,0:T(8,128)(2,1)} %param.16) | copy-start | bytes 9830404
  6.6 401.6 %all-gather.8.cloned.1.call-start = ((), (), s32[]{:S(2)}) async-start(), calls=%async_computation.3 | async-start | bytes 13516800 | tf_op jit(solution)/shard_map/all_gather | solution.py:178
  8.6 411.2 %all-gather.14.cloned.1.call-start = ((), (), s32[]{:S(2)}) async-start(), calls=%async_computation.6 | async-start | bytes 27033600 | tf_op jit(solution)/shard_map/all_gather | solution.py:178
  17.9 429.1 %all-gather.10.cloned.1.call-start = ((), (), s32[]{:S(2)}) async-start(), calls=%async_computation.4 | async-start | bytes 27033600 | tf_op jit(solution)/shard_map/all_gather | solution.py:178
  20.2 454.1 %all-gather.12.cloned.1.call-start = ((), (), s32[]{:S(2)}) async-start(), calls=%async_computation.5 | async-start | bytes 27033600 | tf_op jit(solution)/shard_map/all_gather | solution.py:178
  28.6 3.3 copy-start.7
  29.6 466.5 %all-gather.16.cloned.1.call-start = ((), (), s32[]{:S(2)}) async-start(), calls=%async_computation.7 | async-start | bytes 27033600 | tf_op jit(solution)/shard_map/all_gather | solution.py:178
  62.6 4.7 copy-start.3
  85.7 6.5 %copy-start.2 = (bf16[2048,640]{1,0:T(8,128)(2,1)S(1)}, bf16[2048,640]{1,0:T(8,128)(2,1)}, u32[]{:S(2)}) copy-start(bf16[2048,640]{1,0:T(8,128)(2,1)} %get-tuple-element.11.k_ref) | copy-start | bytes 7864324
  85.7 68.4 %all-to-all-start = ((bf16[8,64,1920]{2,1,0:T(8,128)(2,1)}), bf16[8,64,1920]{2,1,0:T(8,128)(2,1)}, u32[]{:S(2)}, u32[]{:S(2)}) async-start(bf16[8,64,1920]{2,1,0:T(8,128)(2,1)} %bitcast.52), calls=%async_computation | async-start | bytes 3932160 | tf_op jit(solution)/shard_map/all_to_all | solution.py:199
  92.3 7.2 %copy-start.6 = (f32[5,513]{1,0:T(8,128)S(1)}, f32[5,513]{1,0:T(8,128)}, u32[]{:S(2)}) copy-start(f32[5,513]{1,0:T(8,128)} %param.12) | copy-start | bytes 30784
  93.5 53.3 %copy-start.4 = (bf16[2048,640]{1,0:T(8,128)(2,1)S(1)}, bf16[2048,640]{1,0:T(8,128)(2,1)}, u32[]{:S(2)}) copy-start(bf16[2048,640]{1,0:T(8,128)(2,1)} %get-tuple-element.12.v_ref) | copy-start | bytes 7864324
  93.5 52.3 %collective-permute-start = (bf16[2,256,640]{2,1,0:T(8,128)(2,1)S(1)}, bf16[2,256,640]{2,1,0:T(8,128)(2,1)S(1)}, u32[]{:S(2)}, u32[]{:S(2)}) collective-permute-start(bf16[2,256,640]{2,1,0:T(8,128)(2,1)S(1)} %get-tuple-element.23), channel_id=1, source_target_pairs={{0,1},{1,2},{2,3},{3,4},{4,5},{5,6},{6,7},{8,9},{9,10},{10,11},{11... | collective-permute-start | bytes 1966088 | tf_op jit(solution)/shard_map/ppermute | solution.py:190
  97.3 49.4 %collective-permute-start.1 = (bf16[2,256,640]{2,1,0:T(8,128)(2,1)S(1)}, bf16[2,256,640]{2,1,0:T(8,128)(2,1)S(1)}, u32[]{:S(2)}, u32[]{:S(2)}) collective-permute-start(bf16[2,256,640]{2,1,0:T(8,128)(2,1)S(1)} %get-tuple-element.24), channel_id=1, source_target_pairs={{1,0},{2,1},{3,2},{4,3},{5,4},{6,5},{7,6},{9,8},{10,9},{11,10},{12... | collective-permute-start | bytes 1966088 | tf_op jit(solution)/shard_map/ppermute | solution.py:191
  198.1 126.2 %all-to-all-start.1 = ((f32[8,64,650]{2,1,0:T(8,128)}), f32[8,64,650]{2,1,0:T(8,128)S(1)}, u32[]{:S(2)}, u32[]{:S(2)}) async-start(f32[8,64,650]{2,1,0:T(8,128)} %bitcast.3), calls=%async_computation.1 | async-start | bytes 3145728 | tf_op jit(solution)/shard_map/all_to_all | solution.py:208
  353.1 1.9 copy-start.5
  357.4 48.3 %all-to-all-start.2 = ((bf16[2,4,256,640]{3,2,0,1:T(8,128)(2,1)}), bf16[2,4,256,640]{3,2,0,1:T(8,128)(2,1)S(1)}, u32[]{:S(2)}, u32[]{:S(2)}) async-start(bf16[2,4,256,640]{3,2,0,1:T(8,128)(2,1)} %copy.18), calls=%async_computation.2 | async-start | bytes 5242880 | tf_op jit(solution)/shard_map/all_to_all | solution.py:226
  361.4 204.5 %all-gather.18.cloned.1.call-start = ((), (), s32[]{:S(2)}) async-start(), calls=%async_computation.8 | async-start | bytes 6553600 | tf_op jit(solution)/shard_map/all_gather | solution.py:242
  419.8 11.1 %copy-start.8 = (bf16[10240,1280]{1,0:T(8,128)(2,1)S(1)}, bf16[10240,1280]{1,0:T(8,128)(2,1)}, u32[]{:S(2)}) copy-start(bf16[10240,1280]{1,0:T(8,128)(2,1)} %all-gather.14.cloned.1.call-done) | copy-start | bytes 78643200
  419.8 11.8 %copy-start.10 = (bf16[512,2560]{1,0:T(8,128)(2,1)S(1)}, bf16[512,2560]{1,0:T(8,128)(2,1)}, u32[]{:S(2)}) copy-start(bf16[512,2560]{1,0:T(8,128)(2,1)} %fusion.24) | copy-start | bytes 7864324
  447.0 8.9 %copy-start.11 = (bf16[512,2560]{1,0:T(8,128)(2,1)S(1)}, bf16[512,2560]{1,0:T(8,128)(2,1)}, u32[]{:S(2)}) copy-start(bf16[512,2560]{1,0:T(8,128)(2,1)} %fusion.24) | copy-start | bytes 7864324
  447.0 12.4 %copy-start.9 = (bf16[10240,1280]{1,0:T(8,128)(2,1)S(1)}, bf16[10240,1280]{1,0:T(8,128)(2,1)}, u32[]{:S(2)}) copy-start(bf16[10240,1280]{1,0:T(8,128)(2,1)} %all-gather.10.cloned.1.call-done) | copy-start | bytes 78643200
  510.6 111.7 %all-gather.20.cloned.1.call-start = ((), (), s32[]{:S(2)}) async-start(), calls=%async_computation.9 | async-start | bytes 6553600 | tf_op jit(solution)/shard_map/all_gather | solution.py:242
  622.4 9.9 %copy-start.1 = (bf16[2560,640]{1,0:T(8,128)(2,1)S(1)}, bf16[2560,640]{1,0:T(8,128)(2,1)}, u32[]{:S(2)}) copy-start(bf16[2560,640]{1,0:T(8,128)(2,1)} %param.16) | copy-start | bytes 9830404
Sparse Core Ops, SparseCore 0:
  9.4 62.8 all-gather.7
  74.4 109.4 all-gather.13
  186.0 104.8 all-gather.9
  292.8 101.2 all-gather.11
  396.0 90.2 all-gather.15
  510.8 55.1 all-gather.17
  567.5 54.8 all-gather.19

commit v2 on v1

v2 whole, which is shorter than its diff:
```python
import functools
import math

import jax
import jax.numpy as jnp
from jax import lax
from jax.experimental import pallas as pl
from jax.experimental.pallas import tpu as pltpu
from jax.sharding import PartitionSpec as P


LOG2E = math.log2(math.e)
NEG_INF = float("-inf")
F32 = jnp.float32
BF16 = jnp.bfloat16


def _dot(lhs, rhs):
    return jnp.dot(lhs, rhs, preferred_element_type=F32)


def _dot_t(lhs, rhs):
    return lax.dot_general(lhs, rhs, (((1,), (1,)), ((), ())), preferred_element_type=F32)


def _proj_kernel(x_ref, *refs):
    x = x_ref[...]
    n_out = len(refs) // 2
    for w_ref, o_ref in zip(refs[:n_out], refs[n_out:]):
        o_ref[...] = _dot(x, w_ref[...]).astype(BF16)


def _project(tokens, *weights):
    rows, depth = tokens.shape
    cols = weights[0].shape[1]
    n_out = len(weights)
    blk = rows // 4
    w_spec = pl.BlockSpec((depth, cols), lambda i: (0, 0), pipeline_mode=pl.Buffered(1))
    o_spec = pl.BlockSpec((blk, cols), lambda i: (i, 0))
    return pl.pallas_call(
        _proj_kernel,
        grid=(rows // blk,),
        in_specs=[pl.BlockSpec((blk, depth), lambda i: (i, 0))] + [w_spec] * n_out,
        out_specs=[o_spec] * n_out,
        out_shape=[jax.ShapeDtypeStruct((rows, cols), BF16)] * n_out,
        cost_estimate=pl.CostEstimate(
            flops=2 * n_out * rows * depth * cols,
            bytes_accessed=2 * (rows * depth + n_out * depth * cols + n_out * rows * cols),
            transcendentals=0,
        ),
    )(tokens, *weights)


def _glob_kernel(scale, n_heads, q_ref, k_ref, v_ref, o_ref):
    hd = q_ref.shape[1] // n_heads
    rows, lanes = q_ref.shape[0], o_ref.shape[1] - q_ref.shape[1]
    lane = lax.broadcasted_iota(jnp.int32, (rows, lanes), 1)
    stats = jnp.zeros((rows, lanes), F32)
    for h in range(n_heads):
        cols = slice(h * hd, (h + 1) * hd)
        scores = _dot_t(q_ref[:, cols], k_ref[:, cols]) * scale
        top = jnp.max(scores, axis=1, keepdims=True)
        probs = jnp.exp2(scores - top)
        total = jnp.sum(probs, axis=1, keepdims=True)
        o_ref[:, cols] = _dot(probs.astype(BF16), v_ref[:, cols])
        stats = jnp.where(lane == h, top, jnp.where(lane == n_heads + h, total, stats))
    o_ref[:, q_ref.shape[1]:] = stats


def _glob_partial(glob_q, keys, values, n_heads, scale):
    n_glob, width = glob_q.shape
    rows = keys.shape[0]
    blk = n_glob // 4
    out_width = width + 128
    kv_spec = pl.BlockSpec((rows, width), lambda i: (0, 0), pipeline_mode=pl.Buffered(1))
    return pl.pallas_call(
        functools.partial(_glob_kernel, scale * LOG2E, n_heads),
        grid=(n_glob // blk,),
        in_specs=[pl.BlockSpec((blk, width), lambda i: (i, 0)), kv_spec, kv_spec],
        out_specs=pl.BlockSpec((blk, out_width), lambda i: (i, 0)),
        out_shape=jax.ShapeDtypeStruct((n_glob, out_width), F32),
        cost_estimate=pl.CostEstimate(
            flops=16 * n_glob * rows * width,
            bytes_accessed=4 * rows * width + 6 * n_glob * width,
            transcendentals=n_glob * rows * n_heads,
        ),
        name="glob_attn",
    )(glob_q, keys, values)


def _local_kernel(
    window, seq_len, scale, n_heads, start_ref, q_ref, k_ref, v_ref, kl_ref, kr_ref, vl_ref, vr_ref,
    gk_ref, gv_ref, rb_ref, gpos_ref, o_ref, k_ext, v_ext, bias_ref,
):
    blk = pl.program_id(0)
    span = 3 * window
    rows_all = k_ref.shape[0]
    hd = q_ref.shape[1] // n_heads

    @pl.when(blk == 0)
    def _():
        for ext, left, mid, right in ((k_ext, kl_ref, k_ref, kr_ref), (v_ext, vl_ref, v_ref, vr_ref)):
            ext[:window] = left[...]
            ext[window:window + rows_all] = mid[...]
            ext[window + rows_all:] = right[...]
        row = lax.broadcasted_iota(jnp.int32, (window, span), 0)
        for h in range(n_heads):
            bias = jnp.broadcast_to(rb_ref[h], (window, span))
            for bit in range(window.bit_length() - 1):
                bias = jnp.where(((row >> bit) & 1) == 1, pltpu.roll(bias, 1 << bit, 1), bias)
            bias_ref[h] = bias

    first = start_ref[0] + blk * window
    key_pos = first - window + lax.broadcasted_iota(jnp.int32, (1, span), 1)
    edge = jnp.where((key_pos >= 0) & (key_pos < seq_len), 0.0, NEG_INF).astype(F32)
    dist = first + lax.broadcasted_iota(jnp.int32, (window, 1), 0) - gpos_ref[...]
    far = jnp.where(jnp.abs(dist) > window, 0.0, NEG_INF).astype(F32)
    rows = pl.ds(pl.multiple_of(blk * window, window), span)
    for h in range(n_heads):
        cols = slice(h * hd, (h + 1) * hd)
        q = q_ref[:, cols]
        win = _dot_t(q, k_ext[rows, cols]) * scale + (bias_ref[h] + edge)
        glob = _dot_t(q, gk_ref[:, cols]) * scale + far
        top = jnp.maximum(jnp.max(win, axis=1, keepdims=True), jnp.max(glob, axis=1, keepdims=True))
        win = jnp.exp2(win - top)
        glob = jnp.exp2(glob - top)
        inv = 1.0 / (jnp.sum(win, axis=1, keepdims=True) + jnp.sum(glob, axis=1, keepdims=True))
        out = _dot((win * inv).astype(BF16), v_ext[rows, cols])
        out = out + _dot((glob * inv).astype(BF16), gv_ref[:, cols])
        o_ref[:, cols] = out.astype(BF16)


def _local_attn(row_start, q, k, v, k_left, k_right, v_left, v_right, glob_k, glob_v, rel_bias, glob_pos, window, seq_len, scale):
    rows, width = q.shape
    n_heads = rel_bias.shape[0]
    n_glob = glob_k.shape[0]
    span = 3 * window
    pad = jnp.full((n_heads, span - rel_bias.shape[1]), NEG_INF, F32)
    bias_rows = jnp.concatenate([rel_bias * LOG2E, pad], axis=1)[:, None, :]

    def whole(array):
        return pl.BlockSpec(array.shape, lambda c, s: (0,) * array.ndim, pipeline_mode=pl.Buffered(1))

    q_spec = pl.BlockSpec((window, width), lambda c, s: (c, 0))
    held = (k, v, k_left, k_right, v_left, v_right, glob_k, glob_v, bias_rows, glob_pos[None, :])
    grid_spec = pltpu.PrefetchScalarGridSpec(
        num_scalar_prefetch=1,
        grid=(rows // window,),
        in_specs=[q_spec] + [whole(array) for array in held],
        out_specs=q_spec,
        scratch_shapes=[
            pltpu.VMEM((rows + 2 * window, width), BF16),
            pltpu.VMEM((rows + 2 * window, width), BF16),
            pltpu.VMEM((n_heads, window, span), F32),
        ],
    )
    return pl.pallas_call(
        functools.partial(_local_kernel, window, seq_len, scale * LOG2E, n_heads),
        grid_spec=grid_spec,
        out_shape=jax.ShapeDtypeStruct((rows, width), BF16),
        cost_estimate=pl.CostEstimate(
            flops=16 * rows * (span + n_glob) * width,
            bytes_accessed=2 * (2 * rows * width + 2 * (rows + 2 * window + n_glob) * width),
            transcendentals=n_heads * rows * (span + n_glob),
        ),
        name="local_attn",
    )(row_start[None], q, *held)


def solution(mesh):
    n_seq = mesh.shape["sp"]
    n_tp = mesh.shape["tp"]
    to_right = [(sender, sender + 1) for sender in range(n_seq - 1)]
    to_left = [(sender + 1, sender) for sender in range(n_seq - 1)]
    to_next = [(sender, (sender + 1) % n_tp) for sender in range(n_tp)]
    to_prev = [(sender, (sender - 1) % n_tp) for sender in range(n_tp)]
    to_twin = [(sender, (sender + n_tp // 2) % n_tp) for sender in range(n_tp)]
    assert n_tp == 4

    def layer(tokens, glob_pos, rel_bias, w_query, w_key, w_value, w_query_glob, w_out, w_up, w_down):
        local_rows, model_dim = tokens.shape
        n_heads, rel_width = rel_bias.shape
        window = (rel_width - 1) // 2
        width = w_query.shape[1]
        hd = width // n_heads
        n_glob = glob_pos.shape[0]
        glob_blk = n_glob // n_seq
        seq_len = local_rows * n_seq
        scale = hd ** -0.5
        sp_index = lax.axis_index("sp")
        tp_index = lax.axis_index("tp")
        row_start = (sp_index * local_rows).astype(jnp.int32)

        def piece(shard):
            part = shard.shape[0] // n_seq
            return lax.dynamic_slice_in_dim(shard, sp_index * part, part, 0)

        out_full = lax.all_gather(piece(w_out), ("tp", "sp"), axis=0, tiled=True)
        up_piece = lax.ppermute(piece(w_up), "tp", to_twin)
        down_piece = lax.ppermute(piece(w_down), "tp", to_twin)
        up_twin = lax.all_gather(up_piece, "sp", axis=0, tiled=True)
        down_twin = lax.all_gather(down_piece, "sp", axis=0, tiled=True)

        slot = glob_pos - row_start
        pick = (slot[:, None] == jnp.arange(local_rows, dtype=jnp.int32)[None, :]).astype(BF16)
        glob_rows = _dot(pick, tokens).astype(BF16)
        glob_rows = lax.all_to_all(glob_rows, "sp", 0, 0, tiled=True)

        k, v = _project(tokens, w_key, w_value)
        (q,) = _project(tokens, w_query)
        k_left = lax.ppermute(k[local_rows - window:], "sp", to_right)
        v_left = lax.ppermute(v[local_rows - window:], "sp", to_right)
        k_right = lax.ppermute(k[:window], "sp", to_left)
        v_right = lax.ppermute(v[:window], "sp", to_left)

        def to_all(block):
            copies = jnp.broadcast_to(block[None], (n_seq,) + block.shape)
            return lax.all_to_all(copies, "sp", 0, 0, tiled=True).reshape(n_seq * block.shape[0], block.shape[1])

        glob_rows = glob_rows.reshape(n_seq, glob_blk, model_dim).astype(F32).sum(axis=0).astype(BF16)
        glob_qkv = jnp.concatenate([_dot(glob_rows, w).astype(BF16) for w in (w_query_glob, w_key, w_value)], axis=1)
        glob_qkv = to_all(glob_qkv)
        glob_q = glob_qkv[:, :width]
        glob_k = glob_qkv[:, width:2 * width]
        glob_v = glob_qkv[:, 2 * width:]

        parts = _glob_partial(glob_q, k, v, n_heads, scale)
        parts = lax.all_to_all(parts, "sp", 0, 0, tiled=True).reshape(n_seq, glob_blk, parts.shape[1])
        part_max = parts[:, :, width:width + n_heads]
        factor = jnp.exp2(part_max - part_max.max(axis=0))
        tot_sum = (parts[:, :, width + n_heads:width + 2 * n_heads] * factor).sum(axis=0)
        part_out = parts[:, :, :width].reshape(n_seq, glob_blk, n_heads, hd)
        tot_out = (part_out * factor[..., None]).sum(axis=0) / tot_sum[..., None]
        glob_out = to_all(tot_out.astype(BF16).reshape(glob_blk, width))

        win_out = _local_attn(
            row_start, q, k, v, k_left, k_right, v_left, v_right, glob_k, glob_v, rel_bias, glob_pos, window, seq_len, scale
        )

        put = jnp.arange(local_rows, dtype=jnp.int32)[:, None] == slot[None, :]
        is_glob = put.any(axis=1, keepdims=True)
        heads_out = jnp.where(is_glob, _dot(put.astype(BF16), glob_out).astype(BF16), win_out)

        blk = local_rows // (2 * n_tp)
        heads_out = heads_out.reshape(2, n_tp, blk, width)
        heads_out = lax.all_to_all(heads_out, "tp", 1, 1, tiled=True)
        attn_rows = heads_out.transpose(0, 2, 1, 3).reshape(2 * blk, n_tp * width)
        own_rows = lax.dynamic_index_in_dim(tokens.reshape(2, n_tp, blk, model_dim), tp_index, 1, keepdims=False)
        own_rows = own_rows.reshape(2 * blk, model_dim)
        hidden = (own_rows.astype(F32) + _dot(attn_rows, out_full)).astype(BF16)

        def act(rows, weight):
            return jax.nn.gelu(_dot(rows, weight)).astype(BF16)

        from_prev = lax.ppermute(hidden[:blk], "tp", to_next)
        from_next = lax.ppermute(hidden[blk:], "tp", to_prev)
        own_act, own_act_twin = act(hidden, w_up), act(hidden, up_twin)
        guests = jnp.concatenate([from_prev, from_next], axis=0)
        guest_part = _dot(act(guests, w_up), w_down) + _dot(act(guests, up_twin), down_twin)
        back_first = lax.ppermute(guest_part[:blk], "tp", to_prev)
        back_second = lax.ppermute(guest_part[blk:], "tp", to_next)
        own_part = _dot(own_act, w_down) + _dot(own_act_twin, down_twin)
        outs = []
        for rows, back in ((slice(0, blk), back_first), (slice(blk, 2 * blk), back_second)):
            out = (hidden[rows].astype(F32) + (own_part[rows] + back)).astype(BF16)
            outs.append(lax.all_gather(out, "tp", axis=0, tiled=True))
        return jnp.concatenate(outs, axis=0)

    row_spec = P(("batch", "sp"), None)
    col_spec = P(None, "tp")
    head_spec = P("tp", None)
    in_specs = (row_spec, P("batch"), head_spec, col_spec, col_spec, col_spec, col_spec, head_spec, col_spec, head_spec)
    return jax.shard_map(layer, mesh=mesh, in_specs=in_specs, out_specs=row_spec, check_vma=False)
```

time: 645 us -> 639 us (level)
  blocking collectives: 111 us -> 0 us
  waiting for transfers between devices: 185 us -> 293 us
  starting transfers between devices: 24.7 us -> 48.2 us
  local copies, waits for them, and re-layouts: 49.3 us -> 36.1 us
  other arithmetic: 30.8 us -> 18.7 us
    all_gather x4 -> x0, blocking collectives: 111 us -> none  [the longest x1 41.1 us: local_layer(): glob_k = lax.all_gather(mine[:, width:2 * width], 'sp', axis=0, tiled=True)]
    ppermute x2 -> x10, waiting for transfers between devices: 46 us -> 129 us  [the longest x1 50.6 us: layer(): up_piece = lax.ppermute(piece(w_up), 'tp', to_twin)]
    ppermute x2 -> x10, starting transfers between devices: 6.02 us -> 24.5 us  [the longest x1 4.92 us: layer(): down_piece = lax.ppermute(piece(w_down), 'tp', to_twin)]
    concatenate x5 -> x2, other arithmetic: 26.4 us -> 9.87 us  [the longest x1 9.85 us: layer(): return jnp.concatenate(outs, axis=0)]
    all_gather x7 -> x5, waiting for transfers between devices: 97.3 us -> 110 us  [the longest x2 110 us: layer(): outs.append(lax.all_gather(out, 'tp', axis=0, tiled=True))]
    all_to_all x3 -> x5, waiting for transfers between devices: 40.8 us -> 53.1 us  [the longest x1 28.4 us: layer(): heads_out = lax.all_to_all(heads_out, 'tp', 1, 1, tiled=True)]
    slice x5, local copies, waits for them, and re-layouts: 21.5 us -> 10.8 us  [the longest x1 5.18 us: layer(): back_first = lax.ppermute(guest_part[:blk], 'tp', to_prev)]
    pallas_call x1, Pallas kernels: 52.7 us -> 44.3 us  [_local_attn(): pl.pallas_call(functools.partial(_local_kernel, window, seq_len, scale *...]
  transfers between devices with their start and end apart: 12 -> 20, of which waited for: 5 -> 9; matrix products, arithmetic and copies ran while one was open for 27% -> 20% of each run, Pallas kernels for 15% -> 15%
where the time goes in v2:
time: 639 us; the launch traced here: 630 us
  waiting for transfers between devices  293 us (46%)
  matrix products  127 us (20%)
  Pallas kernels  93 us (15%)
  starting transfers between devices  48.2 us (8%)
  local copies, waits for them, and re-layouts  36.1 us (6%)
  other arithmetic  18.7 us (3%)
  between operations  14 us (2%)
    dot_general x12, matrix products, _dot(): return jnp.dot(lhs, rhs, preferred_element_type=F32)  127 us
    all_gather x2, waiting for transfers between devices, layer(): outs.append(lax.all_gather(out, 'tp', axis=0, tiled=True))  110 us
    ppermute x1, waiting for transfers between devices, layer(): up_piece = lax.ppermute(piece(w_up), 'tp', to_twin)  50.6 us
    pallas_call x1, Pallas kernels, _local_attn(): pl.pallas_call(functools.partial(_local_kernel, window, seq_len, scale *...  44.3 us
    ppermute x1, waiting for transfers between devices, layer(): down_piece = lax.ppermute(piece(w_down), 'tp', to_twin)  42.2 us
    pallas_call x2, Pallas kernels, _project(): pl.pallas_call(_proj_kernel, grid=(rows // blk,), in_specs=[pl.BlockSpec(...  34.1 us
    ppermute x1, waiting for transfers between devices, layer(): back_first = lax.ppermute(guest_part[:blk], 'tp', to_prev)  28.6 us
    all_to_all x1, waiting for transfers between devices, layer(): heads_out = lax.all_to_all(heads_out, 'tp', 1, 1, tiled=True)  28.4 us
  transfers between devices with their start and end apart: 20, of which 9 were waited for; matrix products, arithmetic and copies ran while one was open for 20% of the time, Pallas kernels for 15%

profile of v2, /device:TPU:97, one launch (start us, length us, event | category | flops | bytes accessed | tf_op | source)
XLA Modules:
  0.0 630.3 jit_solution(9073490725425594554)
XLA Ops:
  6.6 1.9 copy-done
  10.9 4.9 collective-permute-start.5
  15.8 42.2 %collective-permute-done.5 = bf16[320,2560]{1,0:T(8,128)(2,1)S(1)} collective-permute-done((bf16[320,2560]{1,0:T(8,128)(2,1)S(1)}, bf16[320,2560]{1,0:T(8,128)(2,1)S(1)}, u32[]{:S(2)}, u32[]{:S(2)}) %collective-permute-start.5) | collective-permute-done | bytes 1638432 | tf_op jit(solution)/shard_map/ppermute | solution.py:200
  59.3 11.0 %convolution_convert_fusion = bf16[512,2560]{1,0:T(8,128)(2,1)} fusion(bf16[2048,2560]{1,0:T(8,128)(2,1)} %x_ref.3, s32[512]{0:T(512)S(1)} %broadcast_subtract_fusion), kind=kOutput, calls=%fused_computation.41 | convolution fusion | flops 5371068416 | bytes 13109248 | tf_op jit(solution)/shard_map/dot_general | solution.py:19
  70.2 5.8 all-to-all-start
  77.7 3.0 collective-permute-start.4
  80.7 50.6 %collective-permute-done.4 = bf16[320,2560]{1,0:T(8,128)(2,1)} collective-permute-done((bf16[320,2560]{1,0:T(8,128)(2,1)S(1)}, bf16[320,2560]{1,0:T(8,128)(2,1)}, u32[]{:S(2)}, u32[]{:S(2)}) %collective-permute-start.4) | collective-permute-done | bytes 1638432 | tf_op jit(solution)/shard_map/ppermute | solution.py:199
  131.8 2.8 convolution_convert_fusion.1
  134.6 2.6 convolution_convert_fusion.2
  139.5 4.7 all-to-all-start.1
  144.2 21.7 %shard_map.100 = (bf16[2048,640]{1,0:T(8,128)(2,1)}, bf16[2048,640]{1,0:T(8,128)(2,1)}) custom-call(bf16[2048,2560]{1,0:T(8,128)(2,1)} %x_ref.3, bf16[2560,640]{1,0:T(8,128)(2,1)} %refs_0_.2, bf16[2560,640]{1,0:T(8,128)(2,1)} %refs_1_.1), custom_call_target="tpu_custom_call" | custom-call | flops 13421772800 | bytes 22282240 | tf_op jit(solution)/shard_map/pallas_call | solution.py:40
  165.9 24.7 %all-to-all-done.1 = bf16[8,64,1920]{2,1,0:T(8,128)(2,1)S(1)} async-done(((bf16[8,64,1920]{2,1,0:T(8,128)(2,1)}), bf16[8,64,1920]{2,1,0:T(8,128)(2,1)S(1)}, u32[]{:S(2)}, u32[]{:S(2)}) %all-to-all-start.1) | async-done | bytes 1966112 | tf_op jit(solution)/shard_map/all_to_all | solution.py:218
  192.0 14.7 %glob_attn.1 = f32[512,768]{1,0:T(8,128)} custom-call(bf16[512,640]{1,0:T(8,128)(2,1)} %get-tuple-element.23.q_ref, bf16[2048,640]{1,0:T(8,128)(2,1)} %get-tuple-element.7.k_ref, bf16[2048,640]{1,0:T(8,128)(2,1)} %get-tuple-element.8.v_ref), custom_call_target="tpu_custom_call" | custom-call | flops 10737418240 | bytes 7208960 | tf_op jit(solution)/shard_map/glob_attn/pallas_call | solution.py:76
  206.7 4.3 all-to-all-start.2
  211.0 2.1 fusion.86
  213.1 3.5 collective-permute-start
  216.6 2.0 collective-permute-start.1
  218.5 2.0 fusion.85
  220.5 3.7 collective-permute-start.2
  224.2 2.2 collective-permute-start.3
  227.5 12.4 %shard_map.101.q_ref = bf16[2048,640]{1,0:T(8,128)(2,1)} custom-call(bf16[2048,2560]{1,0:T(8,128)(2,1)} %x_ref.3, bf16[2560,640]{1,0:T(8,128)(2,1)} %refs_0_.3), custom_call_target="tpu_custom_call" | custom-call | flops 6710886400 | bytes 16384000 | tf_op jit(solution)/shard_map/pallas_call | solution.py:40
  240.1 2.0 mul.79
  242.1 2.0 mul.80
  245.3 4.9 all-to-all-start.3
  250.3 44.3 %local_attn.1 = bf16[2048,640]{1,0:T(8,128)(2,1)} custom-call(s32[1]{0:T(128)} %bitcast.6.start_ref, bf16[2048,640]{1,0:T(8,128)(2,1)} %shard_map.101.q_ref, bf16[2048,640]{1,0:T(8,128)(2,1)} %get-tuple-element.7.k_ref, bf16[2048,640]{1,0:T(8,128)(2,1)} %get-tuple-element.8.v_ref, bf16[256,640]{1,0:T(8,128)(2,1)} %collective-permute-done.kl_ref, ...), custom_call_target="tpu_custom_call" | custom-call | flops 26843545600 | bytes 13107200 | tf_op jit(solution)/shard_map/local_attn/pallas_call | solution.py:157
  294.6 1.9 fusion.35
  298.8 3.7 all-to-all-start.4
  302.7 3.5 constant_dynamic-slice_fusion.3
  306.2 28.4 %all-to-all-done.4 = bf16[2,4,256,640]{3,2,0,1:T(8,128)(2,1)S(1)} async-done(((bf16[2,4,256,640]{3,2,0,1:T(8,128)(2,1)}), bf16[2,4,256,640]{3,2,0,1:T(8,128)(2,1)S(1)}, u32[]{:S(2)}, u32[]{:S(2)}) %all-to-all-start.4) | async-done | bytes 2621472 | tf_op jit(solution)/shard_map/all_to_all | solution.py:246
  334.6 2.0 copy.19
  336.7 2.0 copy.22
  338.6 11.1 %fusion.32 = bf16[512,2560]{1,0:T(8,128)(2,1)S(1)} fusion(bf16[512,2560]{1,0:T(8,128)(2,1)} %bitcast.65, bf16[512,2560]{1,0:T(8,128)(2,1)} %bitcast.64, bf16[2560,2560]{1,0:T(8,128)(2,1)} %all-gather.6.cloned.1.call-done), kind=kOutput, calls=%fused_computation.38 | convolution fusion | flops 6714818560 | bytes 20971520 | tf_op jit(solution)/shard_map/dot_general | solution.py:19
  350.3 2.4 collective-permute-start.7
  352.7 10.3 %fusion.88 = f32[512,2560]{1,0:T(8,128)S(1)} fusion(bf16[512,2560]{1,0:T(8,128)(2,1)S(1)} %fusion.32, bf16[2560,2560]{1,0:T(8,128)(2,1)} %param.18), kind=kOutput, calls=%fused_computation.115 | convolution fusion | flops 6710886400 | bytes 20971520 | tf_op jit(solution)/shard_map/dot_general | solution.py:19
  363.0 13.6 %fusion.40 = f32[512,2560]{1,0:T(8,128)} fusion(bf16[2560,2560]{1,0:T(8,128)(2,1)} %param.19, f32[512,2560]{1,0:T(8,128)S(1)} %fusion.88), kind=kOutput, calls=%fused_computation.48 | convolution fusion | flops 6722682880 | bytes 23592960 | tf_op jit(solution)/shard_map/dot_general | solution.py:19
  376.6 4.2 collective-permute-done.6
  382.5 7.0 %fusion.90 = f32[512,2560]{1,0:T(8,128)S(1)} fusion(bf16[512,2560]{1,0:T(8,128)(2,1)S(1)} %constant_dynamic-update-slice_fusion, bf16[2560,2560]{1,0:T(8,128)(2,1)S(1)} %bitcast.71), kind=kOutput, calls=%fused_computation.117 | convolution fusion | flops 6710886400 | bytes 20971520 | tf_op jit(solution)/shard_map/dot_general | solution.py:19
  389.4 13.6 %fusion.37 = f32[512,2560]{1,0:T(8,128)} fusion(bf16[2560,2560]{1,0:T(8,128)(2,1)} %param.19, f32[512,2560]{1,0:T(8,128)S(1)} %fusion.90), kind=kOutput, calls=%fused_computation.47 | convolution fusion | flops 6722682880 | bytes 23592960 | tf_op jit(solution)/shard_map/dot_general | solution.py:19
  403.1 26.7 %convolution_add_fusion = f32[512,2560]{1,0:T(8,128)} fusion(f32[512,2560]{1,0:T(8,128)} %fusion.37, bf16[2560,2560]{1,0:T(8,128)(2,1)} %all-gather.10.cloned.1.call-done, bf16[512,2560]{1,0:T(8,128)(2,1)} %copy-done.5, bf16[2560,2560]{1,0:T(8,128)(2,1)} %all-gather.8.cloned.1.call-done), kind=kOutput, calls=%fused_computation.39 | convolution fusion | flops 13434880000 | bytes 39321600 | tf_op jit(solution)/shard_map/dot_general | solution.py:19
  429.8 5.2 fusion.83
  435.0 2.3 collective-permute-start.8
  437.5 26.0 %convolution_add_fusion.1 = f32[512,2560]{1,0:T(8,128)} fusion(f32[512,2560]{1,0:T(8,128)} %fusion.40, bf16[2560,2560]{1,0:T(8,128)(2,1)} %all-gather.10.cloned.1.call-done, bf16[512,2560]{1,0:T(8,128)(2,1)S(1)} %fusion.32, bf16[2560,2560]{1,0:T(8,128)(2,1)} %all-gather.8.cloned.1.call-done), kind=kOutput, calls=%fused_computation.40 | convolution fusion | flops 13434880000 | bytes 39321600 | tf_op jit(solution)/shard_map/dot_general | solution.py:19
  463.5 28.6 %collective-permute-done.8 = f32[256,2560]{1,0:T(8,128)} collective-permute-done((f32[256,2560]{1,0:T(8,128)}, f32[256,2560]{1,0:T(8,128)}, u32[]{:S(2)}, u32[]{:S(2)}) %collective-permute-start.8) | collective-permute-done | bytes 2621472 | tf_op jit(solution)/shard_map/ppermute | solution.py:260
  492.1 3.2 collective-permute-done.9
  495.3 7.1 %fusion.45 = (bf16[256,2560]{1,0:T(8,128)(2,1)}, bf16[256,2560]{1,0:T(8,128)(2,1)}) fusion(f32[256,2560]{1,0:T(8,128)} %collective-permute-done.8, f32[512,2560]{1,0:T(8,128)} %convolution_add_fusion.1, bf16[512,2560]{1,0:T(8,128)(2,1)S(1)} %fusion.32, f32[256,2560]{1,0:T(8,128)} %collective-permute-done.9), kind=kLoop, calls=%fused_computation.54 | loop fusion | flops 5242880 | bytes 15728640 | tf_op jit(solution)/shard_map/convert_element_type | solution.py:265
  503.1 54.1 %all-gather.14.cloned.1.call-done = bf16[1024,2560]{1,0:T(8,128)(2,1)} async-done(((bf16[256,2560]{1,0:T(8,128)(2,1)}), bf16[1024,2560]{1,0:T(8,128)(2,1)}) %all-gather.14.cloned.1.call-update) | async-done | bytes 5242896 | tf_op jit(solution)/shard_map/all_gather | solution.py:266
  557.1 56.3 %all-gather.12.cloned.1.call-done = bf16[1024,2560]{1,0:T(8,128)(2,1)} async-done(((bf16[256,2560]{1,0:T(8,128)(2,1)}), bf16[1024,2560]{1,0:T(8,128)(2,1)}) %all-gather.12.cloned.1.call-update) | async-done | bytes 5242896 | tf_op jit(solution)/shard_map/all_gather | solution.py:266
  613.5 9.8 %pad_maximum_fusion = bf16[2048,2560]{1,0:T(8,128)(2,1)} fusion(bf16[1024,2560]{1,0:T(8,128)(2,1)} %all-gather.14.cloned.1.call-done, bf16[1024,2560]{1,0:T(8,128)(2,1)} %all-gather.12.cloned.1.call-done), kind=kLoop, calls=%fused_computation | loop fusion | flops 20971520 | bytes 20971520 | tf_op jit(solution)/shard_map/concatenate | solution.py:267
  (71 shorter events, 17.6 us)
Async XLA Ops:
  6.5 1.9 copy-start
  6.6 52.7 %copy-start.7 = (s32[512]{0:T(512)S(1)}, s32[512]{0:T(512)}, u32[]{:S(2)}) copy-start(s32[512]{0:T(512)} %param.11) | copy-start | bytes 6148
  6.6 332.1 %all-gather.6.cloned.1.call-start = ((), (), s32[]{:S(2)}) async-start(), calls=%async_computation.5 | async-start | bytes 13516800 | tf_op jit(solution)/shard_map/all_gather | solution.py:198
  9.3 393.8 %all-gather.10.cloned.1.call-start = ((), (), s32[]{:S(2)}) async-start(), calls=%async_computation.7 | async-start | bytes 14745600 | tf_op jit(solution)/shard_map/all_gather | solution.py:202
  10.9 47.1 %collective-permute-start.5 = (bf16[320,2560]{1,0:T(8,128)(2,1)S(1)}, bf16[320,2560]{1,0:T(8,128)(2,1)S(1)}, u32[]{:S(2)}, u32[]{:S(2)}) collective-permute-start(bf16[320,2560]{1,0:T(8,128)(2,1)S(1)} %constant_dynamic-slice_fusion), channel_id=1, source_target_pairs={{0,16},{8,24},{16,0},{24,8},{1,17},{9,25},{17,1},{25,9},{2,18},{10... | collective-permute-start | bytes 4915208 | tf_op jit(solution)/shard_map/ppermute | solution.py:200
  58.0 1.2 copy-start.4
  70.2 61.2 %all-to-all-start = ((bf16[8,64,2560]{2,1,0:T(8,128)(2,1)}), bf16[8,64,2560]{2,1,0:T(8,128)(2,1)S(1)}, u32[]{:S(2)}, u32[]{:S(2)}) async-start(bf16[8,64,2560]{2,1,0:T(8,128)(2,1)} %bitcast.63), calls=%async_computation | async-start | bytes 5242880 | tf_op jit(solution)/shard_map/all_to_all | solution.py:207
  76.0 327.1 %all-gather.8.cloned.1.call-start = ((), (), s32[]{:S(2)}) async-start(), calls=%async_computation.6 | async-start | bytes 14745600 | tf_op jit(solution)/shard_map/all_gather | solution.py:201
  77.7 53.6 %collective-permute-start.4 = (bf16[320,2560]{1,0:T(8,128)(2,1)S(1)}, bf16[320,2560]{1,0:T(8,128)(2,1)}, u32[]{:S(2)}, u32[]{:S(2)}) collective-permute-start(bf16[320,2560]{1,0:T(8,128)(2,1)S(1)} %constant_dynamic-slice_fusion.1), channel_id=1, source_target_pairs={{0,16},{8,24},{16,0},{24,8},{1,17},{9,25},{17,1},{25,9},{2,18},{10... | collective-permute-start | bytes 4915208 | tf_op jit(solution)/shard_map/ppermute | solution.py:199
  131.8 5.4 copy-start.2
  139.5 51.2 %all-to-all-start.1 = ((bf16[8,64,1920]{2,1,0:T(8,128)(2,1)}), bf16[8,64,1920]{2,1,0:T(8,128)(2,1)S(1)}, u32[]{:S(2)}, u32[]{:S(2)}) async-start(bf16[8,64,1920]{2,1,0:T(8,128)(2,1)} %broadcast_in_dim.16), calls=%async_computation.1 | async-start | bytes 3932160 | tf_op jit(solution)/shard_map/all_to_all | solution.py:218
  206.7 19.7 %copy-start.6 = (f32[5,513]{1,0:T(8,128)S(1)}, f32[5,513]{1,0:T(8,128)}, u32[]{:S(2)}) copy-start(f32[5,513]{1,0:T(8,128)} %param.12) | copy-start | bytes 30784
  206.7 33.2 %all-to-all-start.2 = ((f32[8,64,768]{2,1,0:T(8,128)}), f32[8,64,768]{2,1,0:T(8,128)S(1)}, u32[]{:S(2)}, u32[]{:S(2)}) async-start(f32[8,64,768]{2,1,0:T(8,128)} %bitcast.66), calls=%async_computation.2 | async-start | bytes 3145728 | tf_op jit(solution)/shard_map/all_to_all | solution.py:228
  213.1 37.2 %collective-permute-start = (bf16[256,640]{1,0:T(8,128)(2,1)}, bf16[256,640]{1,0:T(8,128)(2,1)}, u32[]{:S(2)}, u32[]{:S(2)}) collective-permute-start(bf16[256,640]{1,0:T(8,128)(2,1)} %get-tuple-element.20), channel_id=1, source_target_pairs={{0,1},{1,2},{2,3},{3,4},{4,5},{5,6},{6,7},{8,9},{9,10},{10,11},{11... | collective-permute-start | bytes 983048 | tf_op jit(solution)/shard_map/ppermute | solution.py:211
  216.6 33.7 %collective-permute-start.1 = (bf16[256,640]{1,0:T(8,128)(2,1)}, bf16[256,640]{1,0:T(8,128)(2,1)}, u32[]{:S(2)}, u32[]{:S(2)}) collective-permute-start(bf16[256,640]{1,0:T(8,128)(2,1)} %get-tuple-element.19), channel_id=1, source_target_pairs={{1,0},{2,1},{3,2},{4,3},{5,4},{6,5},{7,6},{9,8},{10,9},{11,10},{12... | collective-permute-start | bytes 983048 | tf_op jit(solution)/shard_map/ppermute | solution.py:213
  220.5 29.7 %collective-permute-start.2 = (bf16[256,640]{1,0:T(8,128)(2,1)}, bf16[256,640]{1,0:T(8,128)(2,1)}, u32[]{:S(2)}, u32[]{:S(2)}) collective-permute-start(bf16[256,640]{1,0:T(8,128)(2,1)} %get-tuple-element.18), channel_id=1, source_target_pairs={{0,1},{1,2},{2,3},{3,4},{4,5},{5,6},{6,7},{8,9},{9,10},{10,11},{11... | collective-permute-start | bytes 983048 | tf_op jit(solution)/shard_map/ppermute | solution.py:212
  224.2 26.1 %collective-permute-start.3 = (bf16[256,640]{1,0:T(8,128)(2,1)}, bf16[256,640]{1,0:T(8,128)(2,1)}, u32[]{:S(2)}, u32[]{:S(2)}) collective-permute-start(bf16[256,640]{1,0:T(8,128)(2,1)} %get-tuple-element.17), channel_id=1, source_target_pairs={{1,0},{2,1},{3,2},{4,3},{5,4},{6,5},{7,6},{9,8},{10,9},{11,10},{12... | collective-permute-start | bytes 983048 | tf_op jit(solution)/shard_map/ppermute | solution.py:214
  245.3 49.2 %all-to-all-start.3 = ((bf16[8,64,640]{2,1,0:T(8,128)(2,1)}), bf16[8,64,640]{2,1,0:T(8,128)(2,1)S(1)}, u32[]{:S(2)}, u32[]{:S(2)}) async-start(bf16[8,64,640]{2,1,0:T(8,128)(2,1)} %broadcast_in_dim.17), calls=%async_computation.3 | async-start | bytes 1310720 | tf_op jit(solution)/shard_map/all_to_all | solution.py:218
  294.5 1.9 copy-start.3
  298.8 35.8 %all-to-all-start.4 = ((bf16[2,4,256,640]{3,2,0,1:T(8,128)(2,1)}), bf16[2,4,256,640]{3,2,0,1:T(8,128)(2,1)S(1)}, u32[]{:S(2)}, u32[]{:S(2)}) async-start(bf16[2,4,256,640]{3,2,0,1:T(8,128)(2,1)} %copy.18), calls=%async_computation.4 | async-start | bytes 5242880 | tf_op jit(solution)/shard_map/all_to_all | solution.py:246
  302.6 254.6 %all-gather.14.cloned.1.call-start = ((), (), s32[]{:S(2)}) async-start(), calls=%async_computation.9 | async-start | bytes 6553600 | tf_op jit(solution)/shard_map/all_gather | solution.py:266
  349.9 30.9 %collective-permute-start.6 = (bf16[256,2560]{1,0:T(8,128)(2,1)S(1)}, bf16[256,2560]{1,0:T(8,128)(2,1)S(1)}, u32[]{:S(2)}, u32[]{:S(2)}) collective-permute-start(bf16[256,2560]{1,0:T(8,128)(2,1)S(1)} %get-tuple-element.16), channel_id=1, source_target_pairs={{0,8},{8,16},{16,24},{24,0},{1,9},{9,17},{17,25},{25,1},{2,10},{10... | collective-permute-start | bytes 3932168 | tf_op jit(solution)/shard_map/ppermute | solution.py:255
  350.3 30.6 %collective-permute-start.7 = (bf16[256,2560]{1,0:T(8,128)(2,1)S(1)}, bf16[256,2560]{1,0:T(8,128)(2,1)S(1)}, u32[]{:S(2)}, u32[]{:S(2)}) collective-permute-start(bf16[256,2560]{1,0:T(8,128)(2,1)S(1)} %get-tuple-element.15), channel_id=1, source_target_pairs={{0,24},{8,0},{16,8},{24,16},{1,25},{9,1},{17,9},{25,17},{2,26},{10... | collective-permute-start | bytes 3932168 | tf_op jit(solution)/shard_map/ppermute | solution.py:256
  352.7 29.8 %slice-start = ((s8[13107200]{0:T(1024)(128)(4,1)}), s8[4194304]{0:T(1024)(128)(4,1)S(1)}, s32[]{:S(2)}) async-start(s8[13107200]{0:T(1024)(128)(4,1)} %bitcast.70), calls=%async_computation.10 | async-start | bytes 8388608
  352.7 29.8 %slice-start.1 = ((s8[13107200]{0:T(1024)(128)(4,1)}), s8[4194304]{0:T(1024)(128)(4,1)S(1)}, s32[]{:S(2)}) async-start(s8[13107200]{0:T(1024)(128)(4,1)} %bitcast.70), calls=%async_computation.11 | async-start | bytes 8388608
  363.0 19.5 %slice-start.2 = ((s8[13107200]{0:T(1024)(128)(4,1)}), s8[4194304]{0:T(1024)(128)(4,1)S(1)}, s32[]{:S(2)}) async-start(s8[13107200]{0:T(1024)(128)(4,1)} %bitcast.70), calls=%async_computation.12 | async-start | bytes 8388608
  363.0 19.5 %slice-start.3 = ((s8[13107200]{0:T(1024)(128)(4,1)}), s8[524288]{0:T(1024)(128)(4,1)S(1)}, s32[]{:S(2)}) async-start(s8[13107200]{0:T(1024)(128)(4,1)} %bitcast.70), calls=%async_computation.13 | async-start | bytes 1048576
  381.0 1.5 copy-start.5
  435.0 57.1 %collective-permute-start.8 = (f32[256,2560]{1,0:T(8,128)}, f32[256,2560]{1,0:T(8,128)}, u32[]{:S(2)}, u32[]{:S(2)}) collective-permute-start(f32[256,2560]{1,0:T(8,128)} %get-tuple-element.13), channel_id=1, source_target_pairs={{0,24},{8,0},{16,8},{24,16},{1,25},{9,1},{17,9},{25,17},{2,26},{10... | collective-permute-start | bytes 7864328 | tf_op jit(solution)/shard_map/ppermute | solution.py:260
  437.3 58.0 %collective-permute-start.9 = (f32[256,2560]{1,0:T(8,128)}, f32[256,2560]{1,0:T(8,128)}, u32[]{:S(2)}, u32[]{:S(2)}) collective-permute-start(f32[256,2560]{1,0:T(8,128)} %get-tuple-element.14), channel_id=1, source_target_pairs={{0,8},{8,16},{16,24},{24,0},{1,9},{9,17},{17,25},{25,1},{2,10},{10... | collective-permute-start | bytes 7864328 | tf_op jit(solution)/shard_map/ppermute | solution.py:261
  502.4 111.1 %all-gather.12.cloned.1.call-start = ((), (), s32[]{:S(2)}) async-start(), calls=%async_computation.8 | async-start | bytes 6553600 | tf_op jit(solution)/shard_map/all_gather | solution.py:266
  613.5 9.9 %copy-start.1 = (bf16[640,2560]{1,0:T(8,128)(2,1)S(1)}, bf16[640,2560]{1,0:T(8,128)(2,1)}, u32[]{:S(2)}) copy-start(bf16[640,2560]{1,0:T(8,128)(2,1)} %param.17) | copy-start | bytes 9830404
Sparse Core Ops, SparseCore 0:
  9.4 108.9 all-gather.5
  120.0 108.5 all-gather.9
  230.2 75.2 all-gather.7
  502.5 54.5 all-gather.13
  558.6 54.8 all-gather.11

commit v3 on v2

--- a/solution.py
+++ b/solution.py
@@ -89,20 +89,24 @@
 
 
 def _local_kernel(
-    window, seq_len, scale, n_heads, start_ref, q_ref, k_ref, v_ref, kl_ref, kr_ref, vl_ref, vr_ref,
+    half, window, seq_len, scale, n_heads, start_ref, q_ref, k_ref, v_ref, kh_ref, vh_ref,
     gk_ref, gv_ref, rb_ref, gpos_ref, o_ref, k_ext, v_ext, bias_ref,
 ):
     blk = pl.program_id(0)
     span = 3 * window
     rows_all = k_ref.shape[0]
+    held = k_ext.shape[0] - window
     hd = q_ref.shape[1] // n_heads
 
     @pl.when(blk == 0)
     def _():
-        for ext, left, mid, right in ((k_ext, kl_ref, k_ref, kr_ref), (v_ext, vl_ref, v_ref, vr_ref)):
-            ext[:window] = left[...]
-            ext[window:window + rows_all] = mid[...]
-            ext[window + rows_all:] = right[...]
+        for ext, mid, halo in ((k_ext, k_ref, kh_ref), (v_ext, v_ref, vh_ref)):
+            if half == 0:
+                ext[:window] = halo[...]
+                ext[window:] = mid[:held]
+            else:
+                ext[:held] = mid[rows_all - held:]
+                ext[held:] = halo[...]
         row = lax.broadcasted_iota(jnp.int32, (window, span), 0)
         for h in range(n_heads):
             bias = jnp.broadcast_to(rb_ref[h], (window, span))
@@ -110,7 +114,7 @@
                 bias = jnp.where(((row >> bit) & 1) == 1, pltpu.roll(bias, 1 << bit, 1), bias)
             bias_ref[h] = bias
 
-    first = start_ref[0] + blk * window
+    first = start_ref[0] + half * (rows_all // 2) + blk * window
     key_pos = first - window + lax.broadcasted_iota(jnp.int32, (1, span), 1)
     edge = jnp.where((key_pos >= 0) & (key_pos < seq_len), 0.0, NEG_INF).astype(F32)
     dist = first + lax.broadcasted_iota(jnp.int32, (window, 1), 0) - gpos_ref[...]
@@ -130,24 +134,22 @@
         o_ref[:, cols] = out.astype(BF16)
 
 
-def _local_attn(row_start, q, k, v, k_left, k_right, v_left, v_right, glob_k, glob_v, rel_bias, glob_pos, window, seq_len, scale):
-    rows, width = q.shape
-    n_heads = rel_bias.shape[0]
+def _local_attn(half, row_start, q, k, v, k_halo, v_halo, glob_k, glob_v, bias_rows, glob_pos, window, seq_len, scale):
+    rows, width = q.shape[0] // 2, q.shape[1]
+    n_heads = bias_rows.shape[0]
     n_glob = glob_k.shape[0]
     span = 3 * window
-    pad = jnp.full((n_heads, span - rel_bias.shape[1]), NEG_INF, F32)
-    bias_rows = jnp.concatenate([rel_bias * LOG2E, pad], axis=1)[:, None, :]
+    n_blk = rows // window
 
     def whole(array):
         return pl.BlockSpec(array.shape, lambda c, s: (0,) * array.ndim, pipeline_mode=pl.Buffered(1))
 
-    q_spec = pl.BlockSpec((window, width), lambda c, s: (c, 0))
-    held = (k, v, k_left, k_right, v_left, v_right, glob_k, glob_v, bias_rows, glob_pos[None, :])
+    held = (k, v, k_halo, v_halo, glob_k, glob_v, bias_rows, glob_pos[None, :])
     grid_spec = pltpu.PrefetchScalarGridSpec(
         num_scalar_prefetch=1,
-        grid=(rows // window,),
-        in_specs=[q_spec] + [whole(array) for array in held],
-        out_specs=q_spec,
+        grid=(n_blk,),
+        in_specs=[pl.BlockSpec((window, width), lambda c, s: (c + half * n_blk, 0))] + [whole(array) for array in held],
+        out_specs=pl.BlockSpec((window, width), lambda c, s: (c, 0)),
         scratch_shapes=[
             pltpu.VMEM((rows + 2 * window, width), BF16),
             pltpu.VMEM((rows + 2 * window, width), BF16),
@@ -155,7 +157,7 @@
         ],
     )
     return pl.pallas_call(
-        functools.partial(_local_kernel, window, seq_len, scale * LOG2E, n_heads),
+        functools.partial(_local_kernel, half, window, seq_len, scale * LOG2E, n_heads),
         grid_spec=grid_spec,
         out_shape=jax.ShapeDtypeStruct((rows, width), BF16),
         cost_estimate=pl.CostEstimate(
@@ -163,8 +165,56 @@
             bytes_accessed=2 * (2 * rows * width + 2 * (rows + 2 * window + n_glob) * width),
             transcendentals=n_heads * rows * (span + n_glob),
         ),
-        name="local_attn",
     )(row_start[None], q, *held)
+
+
+def _mlp_kernel(n_steps, x_ref, up_ref, down_ref, *refs):
+    o_ref, act_ref = refs[-2:]
+    step = pl.program_id(0)
+
+    def rise():
+        return jax.nn.gelu(_dot(x_ref[...], up_ref[...])).astype(BF16)
+
+    @pl.when(step == 0)
+    def _():
+        act_ref[...] = rise()
+        o_ref[...] = refs[0][...] if len(refs) == 3 else jnp.zeros_like(o_ref)
+
+    @pl.when((step > 0) & (step < n_steps))
+    def _():
+        last = act_ref[...]
+        o_ref[...] += _dot(last, down_ref[...])
+        act_ref[...] = rise()
+
+    @pl.when(step == n_steps)
+    def _():
+        o_ref[...] += _dot(act_ref[...], down_ref[...])
+
+
+def _mlp(x, w_up, w_down, start=None):
+    rows, depth = x.shape
+    hidden = w_up.shape[1]
+    n_steps = 5 if hidden % 640 == 0 else 2
+    blk = hidden // n_steps
+    whole = pl.BlockSpec((rows, depth), lambda i: (0, 0), pipeline_mode=pl.Buffered(1))
+    return pl.pallas_call(
+        functools.partial(_mlp_kernel, n_steps),
+        grid=(n_steps + 1,),
+        in_specs=[
+            whole,
+            pl.BlockSpec((depth, blk), lambda i: (0, jnp.minimum(i, n_steps - 1))),
+            pl.BlockSpec((blk, depth), lambda i: (jnp.maximum(i - 1, 0), 0)),
+        ]
+        + ([] if start is None else [whole]),
+        out_specs=pl.BlockSpec((rows, depth), lambda i: (0, 0)),
+        out_shape=jax.ShapeDtypeStruct((rows, depth), F32),
+        scratch_shapes=[pltpu.VMEM((rows, blk), BF16)],
+        cost_estimate=pl.CostEstimate(
+            flops=4 * rows * depth * hidden,
+            bytes_accessed=4 * depth * hidden + 6 * rows * depth,
+            transcendentals=rows * hidden,
+        ),
+    )(x, w_up, w_down, *(() if start is None else (start,)))
 
 
 def solution(mesh):
@@ -203,7 +253,8 @@
 
         slot = glob_pos - row_start
         pick = (slot[:, None] == jnp.arange(local_rows, dtype=jnp.int32)[None, :]).astype(BF16)
-        glob_rows = _dot(pick, tokens).astype(BF16)
+        share = model_dim // n_tp
+        glob_rows = _dot(pick, lax.dynamic_slice_in_dim(tokens, tp_index * share, share, 1)).astype(BF16)
         glob_rows = lax.all_to_all(glob_rows, "sp", 0, 0, tiled=True)
 
         k, v = _project(tokens, w_key, w_value)
@@ -213,13 +264,15 @@
         k_right = lax.ppermute(k[:window], "sp", to_left)
         v_right = lax.ppermute(v[:window], "sp", to_left)
 
-        def to_all(block):
-            copies = jnp.broadcast_to(block[None], (n_seq,) + block.shape)
-            return lax.all_to_all(copies, "sp", 0, 0, tiled=True).reshape(n_seq * block.shape[0], block.shape[1])
-
-        glob_rows = glob_rows.reshape(n_seq, glob_blk, model_dim).astype(F32).sum(axis=0).astype(BF16)
+        def to_all(block, axes, size):
+            copies = jnp.broadcast_to(block[None], (size,) + block.shape)
+            return lax.all_to_all(copies, axes, 0, 0, tiled=True)
+
+        glob_rows = glob_rows.reshape(n_seq, glob_blk, share).astype(F32).sum(axis=0).astype(BF16)
+        glob_rows = to_all(glob_rows, "tp", n_tp)
+        glob_rows = glob_rows.transpose(1, 0, 2).reshape(glob_blk, model_dim)
         glob_qkv = jnp.concatenate([_dot(glob_rows, w).astype(BF16) for w in (w_query_glob, w_key, w_value)], axis=1)
-        glob_qkv = to_all(glob_qkv)
+        glob_qkv = to_all(glob_qkv, "sp", n_seq).reshape(n_glob, 3 * width)
         glob_q = glob_qkv[:, :width]
         glob_k = glob_qkv[:, width:2 * width]
         glob_v = glob_qkv[:, 2 * width:]
@@ -231,38 +284,52 @@
         tot_sum = (parts[:, :, width + n_heads:width + 2 * n_heads] * factor).sum(axis=0)
         part_out = parts[:, :, :width].reshape(n_seq, glob_blk, n_heads, hd)
         tot_out = (part_out * factor[..., None]).sum(axis=0) / tot_sum[..., None]
-        glob_out = to_all(tot_out.astype(BF16).reshape(glob_blk, width))
-
-        win_out = _local_attn(
-            row_start, q, k, v, k_left, k_right, v_left, v_right, glob_k, glob_v, rel_bias, glob_pos, window, seq_len, scale
-        )
-
-        put = jnp.arange(local_rows, dtype=jnp.int32)[:, None] == slot[None, :]
-        is_glob = put.any(axis=1, keepdims=True)
-        heads_out = jnp.where(is_glob, _dot(put.astype(BF16), glob_out).astype(BF16), win_out)
-
+        glob_out = to_all(tot_out.astype(BF16).reshape(glob_blk, width), ("tp", "sp"), n_tp * n_seq)
+        glob_out = glob_out.reshape(n_tp, n_glob, width).transpose(1, 0, 2).reshape(n_glob, n_tp * width)
+
+        pad = jnp.full((n_heads, 3 * window - rel_width), NEG_INF, F32)
+        bias_rows = jnp.concatenate([rel_bias * LOG2E, pad], axis=1)[:, None, :]
         blk = local_rows // (2 * n_tp)
-        heads_out = heads_out.reshape(2, n_tp, blk, width)
-        heads_out = lax.all_to_all(heads_out, "tp", 1, 1, tiled=True)
-        attn_rows = heads_out.transpose(0, 2, 1, 3).reshape(2 * blk, n_tp * width)
-        own_rows = lax.dynamic_index_in_dim(tokens.reshape(2, n_tp, blk, model_dim), tp_index, 1, keepdims=False)
-        own_rows = own_rows.reshape(2 * blk, model_dim)
-        hidden = (own_rows.astype(F32) + _dot(attn_rows, out_full)).astype(BF16)
-
-        def act(rows, weight):
-            return jax.nn.gelu(_dot(rows, weight)).astype(BF16)
-
-        from_prev = lax.ppermute(hidden[:blk], "tp", to_next)
-        from_next = lax.ppermute(hidden[blk:], "tp", to_prev)
-        own_act, own_act_twin = act(hidden, w_up), act(hidden, up_twin)
-        guests = jnp.concatenate([from_prev, from_next], axis=0)
-        guest_part = _dot(act(guests, w_up), w_down) + _dot(act(guests, up_twin), down_twin)
-        back_first = lax.ppermute(guest_part[:blk], "tp", to_prev)
-        back_second = lax.ppermute(guest_part[blk:], "tp", to_next)
-        own_part = _dot(own_act, w_down) + _dot(own_act_twin, down_twin)
+        own_tokens = lax.dynamic_index_in_dim(tokens.reshape(2, n_tp, blk, model_dim), tp_index, 1, keepdims=False)
+        hidden = []
+        for half, (k_halo, v_halo) in enumerate(((k_left, v_left), (k_right, v_right))):
+            win_out = _local_attn(
+                half, row_start, q, k, v, k_halo, v_halo, glob_k, glob_v, bias_rows, glob_pos, window, seq_len, scale
+            )
+            win_out = win_out.reshape(n_tp, blk, width)
+            held = [lax.dynamic_index_in_dim(win_out, tp_index, 0, keepdims=False)]
+            for shift in range(1, n_tp):
+                sent = lax.dynamic_index_in_dim(win_out, lax.rem(tp_index + shift, n_tp), 0, keepdims=False)
+                held.append(lax.ppermute(sent, "tp", [(i, (i + shift) % n_tp) for i in range(n_tp)]))
+            held = jnp.stack(held)
+            win_out = jnp.concatenate(
+                [
+                    lax.dynamic_index_in_dim(held, lax.rem(tp_index - source + n_tp, n_tp), 0, keepdims=False)
+                    for source in range(n_tp)
+                ],
+                axis=1,
+            )
+            first = row_start + half * (local_rows // 2) + tp_index * blk
+            put = (first + jnp.arange(blk, dtype=jnp.int32))[:, None] == glob_pos[None, :]
+            attn_rows = jnp.where(
+                put.any(axis=1, keepdims=True), _dot(put.astype(BF16), glob_out).astype(BF16), win_out
+            )
+            hidden.append((own_tokens[half].astype(F32) + _dot(attn_rows, out_full)).astype(BF16))
+
+        there, home = (to_next, to_prev), (to_prev, to_next)
+        guests = []
+        for half in range(2):
+            guests.append(lax.ppermute(hidden[half], "tp", there[half]))
+        own_part = [_mlp(hidden[half], w_up, w_down) for half in range(2)]
+        back = []
+        for half in range(2):
+            guest_part = _mlp(guests[half], w_up, w_down)
+            guest_part = _mlp(guests[half], up_twin, down_twin, guest_part)
+            back.append(lax.ppermute(guest_part, "tp", home[half]))
         outs = []
-        for rows, back in ((slice(0, blk), back_first), (slice(blk, 2 * blk), back_second)):
-            out = (hidden[rows].astype(F32) + (own_part[rows] + back)).astype(BF16)
+        for half in range(2):
+            part = _mlp(hidden[half], up_twin, down_twin, own_part[half])
+            out = (hidden[half].astype(F32) + (part + back[half])).astype(BF16)
             outs.append(lax.all_gather(out, "tp", axis=0, tiled=True))
         return jnp.concatenate(outs, axis=0)
 

time: 639 us -> 749 us (1.17)
  Pallas kernels: 93 us -> 226 us
  matrix products: 127 us -> 28.4 us
  waiting for transfers between devices: 293 us -> 341 us
  blocking collectives: 0 us -> 31.9 us
    pallas_call x1 -> x10, Pallas kernels: 44.3 us -> 177 us  [the longest x8 122 us: _mlp(): pl.pallas_call(functools.partial(_mlp_kernel, n_steps), grid=(n_steps + 1...]
    dot_general x12 -> x6, matrix products: 127 us -> 28.4 us  [_dot(): return jnp.dot(lhs, rhs, preferred_element_type=F32)]
    ppermute x4 -> x10, waiting for transfers between devices: 36 us -> 127 us  [the longest x2 82.4 us: layer(): guests.append(lax.ppermute(hidden[half], 'tp', there[half]))]
    all_gather x2, waiting for transfers between devices: 110 us -> 57.8 us  [layer(): outs.append(lax.all_gather(out, 'tp', axis=0, tiled=True))]
    all_to_all x0 -> x2, blocking collectives: none -> 31.9 us  [the longest x1 21 us: layer(): glob_rows = lax.all_to_all(glob_rows, 'sp', 0, 0, tiled=True)]
    all_to_all x4 -> x2, waiting for transfers between devices: 53.1 us -> 24.8 us  [to_all(): return lax.all_to_all(copies, axes, 0, 0, tiled=True)]
    all_to_all x1, waiting for transfers between devices: 0.01 us -> 27.6 us  [layer(): lax.all_to_all(parts, 'sp', 0, 0, tiled=True)]
    ppermute x1, waiting for transfers between devices: 50.6 us -> 61.3 us  [layer(): up_piece = lax.ppermute(piece(w_up), 'tp', to_twin)]
  transfers between devices with their start and end apart: 20 -> 24, of which waited for: 9 -> 11; matrix products, arithmetic and copies ran while one was open for 20% -> 8% of each run, Pallas kernels for 15% -> 30%
where the time goes in v3:
time: 749 us; the launch traced here: 740 us
  waiting for transfers between devices  341 us (46%)
  Pallas kernels  226 us (30%)
  starting transfers between devices  47.1 us (6%)
  blocking collectives  31.9 us (4%)
  local copies, waits for them, and re-layouts  31.8 us (4%)
  matrix products  28.4 us (4%)
  other arithmetic  20.3 us (3%)
  between operations  14.1 us (2%)
    pallas_call x8, Pallas kernels, _mlp(): pl.pallas_call(functools.partial(_mlp_kernel, n_steps), grid=(n_steps + 1...  122 us
    ppermute x2, waiting for transfers between devices, layer(): guests.append(lax.ppermute(hidden[half], 'tp', there[half]))  82.4 us
    ppermute x1, waiting for transfers between devices, layer(): up_piece = lax.ppermute(piece(w_up), 'tp', to_twin)  61.3 us
    all_gather x2, waiting for transfers between devices, layer(): outs.append(lax.all_gather(out, 'tp', axis=0, tiled=True))  57.8 us
    pallas_call x2, Pallas kernels, _local_attn(): pl.pallas_call(functools.partial(_local_kernel, half, window, seq_len, sc...  55.4 us
    ppermute x1, waiting for transfers between devices, layer(): down_piece = lax.ppermute(piece(w_down), 'tp', to_twin)  42.2 us
    pallas_call x2, Pallas kernels, _project(): pl.pallas_call(_proj_kernel, grid=(rows // blk,), in_specs=[pl.BlockSpec(...  34 us
    dot_general x6, matrix products, _dot(): return jnp.dot(lhs, rhs, preferred_element_type=F32)  28.4 us
  transfers between devices with their start and end apart: 24, of which 11 were waited for; matrix products, arithmetic and copies ran while one was open for 8% of the time, Pallas kernels for 30%

profile of v3, /device:TPU:97, one launch (start us, length us, event | category | flops | bytes accessed | tf_op | source)
XLA Modules:
  0.0 740.1 jit_solution(18085438714421492122)
XLA Ops:
  10.9 4.9 collective-permute-start.6
  15.9 42.2 %collective-permute-done.6 = bf16[320,2560]{1,0:T(8,128)(2,1)S(1)} collective-permute-done((bf16[320,2560]{1,0:T(8,128)(2,1)S(1)}, bf16[320,2560]{1,0:T(8,128)(2,1)S(1)}, u32[]{:S(2)}, u32[]{:S(2)}) %collective-permute-start.6) | collective-permute-done | bytes 1638432 | tf_op jit(solution)/shard_map/ppermute | solution.py:250
  60.9 2.8 collective-permute-start.5
  63.6 61.3 %collective-permute-done.5 = bf16[320,2560]{1,0:T(8,128)(2,1)S(1)} collective-permute-done((bf16[320,2560]{1,0:T(8,128)(2,1)S(1)}, bf16[320,2560]{1,0:T(8,128)(2,1)S(1)}, u32[]{:S(2)}, u32[]{:S(2)}) %collective-permute-start.5) | collective-permute-done | bytes 1638432 | tf_op jit(solution)/shard_map/ppermute | solution.py:249
  126.3 3.7 fusion.7
  130.0 21.0 %all_to_all.33 = bf16[8,64,640]{2,1,0:T(8,128)(2,1)S(1)} all-to-all(bf16[8,64,640]{2,1,0:T(8,128)(2,1)S(1)} %bitcast.86), channel_id=1, replica_groups=mesh['batch'=1,'tp'=4,'sp'=8] {'sp'}, dimensions={0} | all-to-all | bytes 1310720 | tf_op jit(solution)/shard_map/all_to_all | solution.py:258
  151.1 10.9 %all_to_all.34 = bf16[4,64,640]{2,1,0:T(8,128)(2,1)S(1)} all-to-all(bf16[4,64,640]{2,1,0:T(8,128)(2,1)S(1)} %broadcast_in_dim.23), channel_id=1, replica_groups=mesh['batch'=1,'tp'=4,'sp'=8] {'tp'}, dimensions={0} | all-to-all | bytes 655360 | tf_op jit(solution)/shard_map/all_to_all | solution.py:269
  162.0 2.7 convolution_convert_fusion.2
  169.1 5.9 all-to-all-start.2
  175.0 21.5 %shard_map.100 = (bf16[2048,640]{1,0:T(8,128)(2,1)}, bf16[2048,640]{1,0:T(8,128)(2,1)}) custom-call(bf16[2048,2560]{1,0:T(8,128)(2,1)} %x_ref.3, bf16[2560,640]{1,0:T(8,128)(2,1)} %refs_0_.2, bf16[2560,640]{1,0:T(8,128)(2,1)} %refs_1_.1), custom_call_target="tpu_custom_call" | custom-call | flops 13421772800 | bytes 22282240 | tf_op jit(solution)/shard_map/pallas_call | solution.py:40
  196.5 24.8 %all-to-all-done.2 = bf16[8,64,1920]{2,1,0:T(8,128)(2,1)S(1)} async-done(((bf16[8,64,1920]{2,1,0:T(8,128)(2,1)}), bf16[8,64,1920]{2,1,0:T(8,128)(2,1)S(1)}, u32[]{:S(2)}, u32[]{:S(2)}) %all-to-all-start.2) | async-done | bytes 1966112 | tf_op jit(solution)/shard_map/all_to_all | solution.py:269
  222.7 14.5 %glob_attn.1 = f32[512,768]{1,0:T(8,128)} custom-call(bf16[512,640]{1,0:T(8,128)(2,1)} %get-tuple-element.19.q_ref, bf16[2048,640]{1,0:T(8,128)(2,1)} %get-tuple-element.7.k_ref, bf16[2048,640]{1,0:T(8,128)(2,1)} %get-tuple-element.8.v_ref), custom_call_target="tpu_custom_call" | custom-call | flops 10737418240 | bytes 7208960 | tf_op jit(solution)/shard_map/glob_attn/pallas_call | solution.py:76
  237.2 4.2 all-to-all-start.3
  241.4 2.0 fusion.29
  243.4 3.5 collective-permute-start
  246.9 2.0 fusion.28
  248.9 2.3 collective-permute-start.1
  251.8 27.6 %all-to-all-done.3 = f32[8,64,768]{2,1,0:T(8,128)S(1)} async-done(((f32[8,64,768]{2,1,0:T(8,128)}), f32[8,64,768]{2,1,0:T(8,128)S(1)}, u32[]{:S(2)}, u32[]{:S(2)}) %all-to-all-start.3) | async-done | bytes 1572896 | tf_op jit(solution)/shard_map/all_to_all | solution.py:281
  279.6 2.0 mul.40
  285.5 3.7 all-to-all-start.4
  289.3 12.5 %shard_map.101.q_ref = bf16[2048,640]{1,0:T(8,128)(2,1)} custom-call(bf16[2048,2560]{1,0:T(8,128)(2,1)} %x_ref.3, bf16[2560,640]{1,0:T(8,128)(2,1)} %refs_0_.3), custom_call_target="tpu_custom_call" | custom-call | flops 6710886400 | bytes 16384000 | tf_op jit(solution)/shard_map/pallas_call | solution.py:40
  301.8 27.7 %shard_map.102 = bf16[1024,640]{1,0:T(8,128)(2,1)} custom-call(s32[1]{0:T(128)} %bitcast.9.start_ref, bf16[2048,640]{1,0:T(8,128)(2,1)} %shard_map.101.q_ref, bf16[2048,640]{1,0:T(8,128)(2,1)} %get-tuple-element.7.k_ref, bf16[2048,640]{1,0:T(8,128)(2,1)} %get-tuple-element.8.v_ref, bf16[256,640]{1,0:T(8,128)(2,1)} %collective-permute-done.kh_ref, ...), custom_call_target="tpu_custom_call" | custom-call | flops 13421772800 | bytes 7864320 | tf_op jit(solution)/shard_map/pallas_call | solution.py:159
  331.0 2.9 collective-permute-start.4
  335.7 6.4 collective-permute-done.4
  342.1 2.6 collective-permute-done.3
  344.8 8.2 %collective-permute-done.2 = bf16[256,640]{1,0:T(8,128)(2,1)S(1)} collective-permute-done((bf16[256,640]{1,0:T(8,128)(2,1)S(1)}, bf16[256,640]{1,0:T(8,128)(2,1)S(1)}, u32[]{:S(2)}, u32[]{:S(2)}) %collective-permute-start.2) | collective-permute-done | bytes 327712 | tf_op jit(solution)/shard_map/ppermute | solution.py:303
  354.3 2.6 copy.15
  356.9 10.6 %fusion.1.x_ref = bf16[256,2560]{1,0:T(8,128)(2,1)S(1)} fusion(bf16[2560,2560]{1,0:T(8,128)(2,1)} %all-gather.6.cloned.1.call-done, bf16[2,4,256,2560]{3,2,1,0:T(8,128)(2,1)} %bitcast.94, s32[]{:T(128)S(6)} %select_n.46, bf16[512,2560]{0,1:T(8,128)(2,1)} %bitcast.79, bf16[256,640]{1,0:T(8,128)(2,1)} %get-tuple-element.21, ...), kind=kOutput, calls=%fused_computation.5 | convolution fusion | flops 4035182592 | bytes 19664132 | tf_op jit(solution)/shard_map/dot_general | solution.py:19
  367.6 2.4 collective-permute-start.9
  372.0 26.6 %collective-permute-done.7.x_ref = bf16[256,2560]{1,0:T(8,128)(2,1)S(1)} collective-permute-done((bf16[256,2560]{1,0:T(8,128)(2,1)S(1)}, bf16[256,2560]{1,0:T(8,128)(2,1)S(1)}, u32[]{:S(2)}, u32[]{:S(2)}) %collective-permute-start.7) | collective-permute-done | bytes 1310752 | tf_op jit(solution)/shard_map/ppermute | solution.py:322
  399.8 14.8 %shard_map.105.refs_0_ = f32[256,2560]{1,0:T(8,128)} custom-call(bf16[256,2560]{1,0:T(8,128)(2,1)} %copy-done.6, bf16[2560,2560]{1,0:T(8,128)(2,1)} %up_ref.7, bf16[2560,2560]{1,0:T(8,128)(2,1)} %down_ref.7), custom_call_target="tpu_custom_call" | custom-call | flops 6710886400 | bytes 30146560 | tf_op jit(solution)/shard_map/pallas_call | solution.py:200
  414.6 15.6 %shard_map.106 = f32[256,2560]{1,0:T(8,128)} custom-call(bf16[256,2560]{1,0:T(8,128)(2,1)} %copy-done.6, bf16[2560,2560]{1,0:T(8,128)(2,1)} %all-gather.8.cloned.1.call-done.up_ref, bf16[2560,2560]{1,0:T(8,128)(2,1)} %all-gather.10.cloned.1.call-done.down_ref, f32[256,2560]{1,0:T(8,128)} %shard_map.105.refs_0_), custom_call_target="tpu_custom_call" | custom-call | flops 6710886400 | bytes 30146560 | tf_op jit(solution)/shard_map/pallas_call | solution.py:200
  430.4 27.6 %shard_map.107 = bf16[1024,640]{1,0:T(8,128)(2,1)} custom-call(s32[1]{0:T(128)} %bitcast.9.start_ref, bf16[2048,640]{1,0:T(8,128)(2,1)} %shard_map.101.q_ref, bf16[2048,640]{1,0:T(8,128)(2,1)} %get-tuple-element.7.k_ref, bf16[2048,640]{1,0:T(8,128)(2,1)} %get-tuple-element.8.v_ref, bf16[256,640]{1,0:T(8,128)(2,1)} %collective-permute-done.9.kh_ref, ...), custom_call_target="tpu_custom_call" | custom-call | flops 13421772800 | bytes 7864320 | tf_op jit(solution)/shard_map/pallas_call | solution.py:159
  459.5 3.2 collective-permute-start.12
  462.9 14.8 %shard_map.103.refs_0_ = f32[256,2560]{1,0:T(8,128)} custom-call(bf16[256,2560]{1,0:T(8,128)(2,1)} %copy-done.2, bf16[2560,2560]{1,0:T(8,128)(2,1)} %up_ref.7, bf16[2560,2560]{1,0:T(8,128)(2,1)} %down_ref.7), custom_call_target="tpu_custom_call" | custom-call | flops 6710886400 | bytes 30146560 | tf_op jit(solution)/shard_map/pallas_call | solution.py:200
  477.7 15.7 %shard_map.104 = f32[256,2560]{1,0:T(8,128)} custom-call(bf16[256,2560]{1,0:T(8,128)(2,1)} %copy-done.2, bf16[2560,2560]{1,0:T(8,128)(2,1)} %all-gather.8.cloned.1.call-done.up_ref, bf16[2560,2560]{1,0:T(8,128)(2,1)} %all-gather.10.cloned.1.call-done.down_ref, f32[256,2560]{1,0:T(8,128)} %shard_map.103.refs_0_), custom_call_target="tpu_custom_call" | custom-call | flops 6710886400 | bytes 30146560 | tf_op jit(solution)/shard_map/pallas_call | solution.py:200
  493.5 4.2 add_convert_fusion.1
  499.2 10.1 %fusion.2.x_ref = bf16[256,2560]{1,0:T(8,128)(2,1)S(1)} fusion(bf16[2560,2560]{1,0:T(8,128)(2,1)} %all-gather.6.cloned.1.call-done, bf16[2,4,256,2560]{3,2,1,0:T(8,128)(2,1)} %bitcast.95, s32[]{:T(128)S(6)} %add.141, s32[]{:T(128)S(6)} %select_n.46, bf16[512,2560]{0,1:T(8,128)(2,1)} %bitcast.80, bf16[256,640]{1,0:T(8,128)(2,1)S(1)} %get-tuple-element.29, ...), kind=kOutput, calls=%fused_computation.6 | convolution fusion | flops 4035182592 | bytes 19664136 | tf_op jit(solution)/shard_map/dot_general | solution.py:19
  509.3 7.0 collective-permute-start.14
  516.3 55.8 %collective-permute-done.14.x_ref = bf16[256,2560]{1,0:T(8,128)(2,1)S(1)} collective-permute-done((bf16[256,2560]{1,0:T(8,128)(2,1)S(1)}, bf16[256,2560]{1,0:T(8,128)(2,1)S(1)}, u32[]{:S(2)}, u32[]{:S(2)}) %collective-permute-start.14) | collective-permute-done | bytes 1310752 | tf_op jit(solution)/shard_map/ppermute | solution.py:322
  573.2 14.8 %shard_map.110.refs_0_ = f32[256,2560]{1,0:T(8,128)} custom-call(bf16[256,2560]{1,0:T(8,128)(2,1)} %copy-done.7, bf16[2560,2560]{1,0:T(8,128)(2,1)} %up_ref.7, bf16[2560,2560]{1,0:T(8,128)(2,1)} %down_ref.7), custom_call_target="tpu_custom_call" | custom-call | flops 6710886400 | bytes 30146560 | tf_op jit(solution)/shard_map/pallas_call | solution.py:200
  588.0 15.6 %shard_map.111 = f32[256,2560]{1,0:T(8,128)} custom-call(bf16[256,2560]{1,0:T(8,128)(2,1)} %copy-done.7, bf16[2560,2560]{1,0:T(8,128)(2,1)} %all-gather.8.cloned.1.call-done.up_ref, bf16[2560,2560]{1,0:T(8,128)(2,1)} %all-gather.10.cloned.1.call-done.down_ref, f32[256,2560]{1,0:T(8,128)} %shard_map.110.refs_0_), custom_call_target="tpu_custom_call" | custom-call | flops 6710886400 | bytes 30146560 | tf_op jit(solution)/shard_map/pallas_call | solution.py:200
  603.6 14.8 %shard_map.108.refs_0_ = f32[256,2560]{1,0:T(8,128)} custom-call(bf16[256,2560]{1,0:T(8,128)(2,1)} %copy-done.4, bf16[2560,2560]{1,0:T(8,128)(2,1)} %up_ref.7, bf16[2560,2560]{1,0:T(8,128)(2,1)} %down_ref.7), custom_call_target="tpu_custom_call" | custom-call | flops 6710886400 | bytes 30146560 | tf_op jit(solution)/shard_map/pallas_call | solution.py:200
  618.4 15.7 %shard_map.109 = f32[256,2560]{1,0:T(8,128)} custom-call(bf16[256,2560]{1,0:T(8,128)(2,1)} %copy-done.4, bf16[2560,2560]{1,0:T(8,128)(2,1)} %all-gather.8.cloned.1.call-done.up_ref, bf16[2560,2560]{1,0:T(8,128)(2,1)} %all-gather.10.cloned.1.call-done.down_ref, f32[256,2560]{1,0:T(8,128)} %shard_map.108.refs_0_), custom_call_target="tpu_custom_call" | custom-call | flops 6710886400 | bytes 30146560 | tf_op jit(solution)/shard_map/pallas_call | solution.py:200
  634.1 27.2 %collective-permute-done.15 = f32[256,2560]{1,0:T(8,128)} collective-permute-done((f32[256,2560]{1,0:T(8,128)}, f32[256,2560]{1,0:T(8,128)}, u32[]{:S(2)}, u32[]{:S(2)}) %collective-permute-start.15) | collective-permute-done | bytes 2621472 | tf_op jit(solution)/shard_map/ppermute | solution.py:328
  661.3 4.2 add_convert_fusion
  665.5 57.7 %all-gather.14.cloned.1.call-done = bf16[1024,2560]{1,0:T(8,128)(2,1)} async-done(((bf16[256,2560]{1,0:T(8,128)(2,1)}), bf16[1024,2560]{1,0:T(8,128)(2,1)}) %all-gather.14.cloned.1.call-update) | async-done | bytes 5242896 | tf_op jit(solution)/shard_map/all_gather | solution.py:333
  723.3 9.8 %pad_maximum_fusion = bf16[2048,2560]{1,0:T(8,128)(2,1)} fusion(bf16[1024,2560]{1,0:T(8,128)(2,1)} %all-gather.14.cloned.1.call-done, bf16[1024,2560]{1,0:T(8,128)(2,1)} %all-gather.12.cloned.1.call-done), kind=kLoop, calls=%fused_computation | loop fusion | flops 20971520 | bytes 20971520 | tf_op jit(solution)/shard_map/concatenate | solution.py:334
  (98 shorter events, 31.3 us)
Async XLA Ops:
  6.5 1.9 copy-start
  6.6 350.4 %all-gather.6.cloned.1.call-start = ((), (), s32[]{:S(2)}) async-start(), calls=%async_computation.5 | async-start | bytes 13516800 | tf_op jit(solution)/shard_map/all_gather | solution.py:248
  9.3 405.2 %all-gather.10.cloned.1.call-start = ((), (), s32[]{:S(2)}) async-start(), calls=%async_computation.7 | async-start | bytes 14745600 | tf_op jit(solution)/shard_map/all_gather | solution.py:252
  10.9 47.1 %collective-permute-start.6 = (bf16[320,2560]{1,0:T(8,128)(2,1)S(1)}, bf16[320,2560]{1,0:T(8,128)(2,1)S(1)}, u32[]{:S(2)}, u32[]{:S(2)}) collective-permute-start(bf16[320,2560]{1,0:T(8,128)(2,1)S(1)} %constant_dynamic-slice_fusion.1), channel_id=1, source_target_pairs={{0,16},{8,24},{16,0},{24,8},{1,17},{9,25},{17,1},{25,9},{2,18},{10... | collective-permute-start | bytes 4915208 | tf_op jit(solution)/shard_map/ppermute | solution.py:250
  58.0 1.2 copy-start.10
  59.2 67.0 %copy-start.15 = (s32[512]{0:T(512)S(1)}, s32[512]{0:T(512)}, u32[]{:S(2)}) copy-start(s32[512]{0:T(512)} %param.11) | copy-start | bytes 6148
  59.2 355.3 %all-gather.8.cloned.1.call-start = ((), (), s32[]{:S(2)}) async-start(), calls=%async_computation.6 | async-start | bytes 14745600 | tf_op jit(solution)/shard_map/all_gather | solution.py:251
  60.9 64.1 %collective-permute-start.5 = (bf16[320,2560]{1,0:T(8,128)(2,1)S(1)}, bf16[320,2560]{1,0:T(8,128)(2,1)S(1)}, u32[]{:S(2)}, u32[]{:S(2)}) collective-permute-start(bf16[320,2560]{1,0:T(8,128)(2,1)S(1)} %constant_dynamic-slice_fusion.2), channel_id=1, source_target_pairs={{0,16},{8,24},{16,0},{24,8},{1,17},{9,25},{17,1},{25,9},{2,18},{10... | collective-permute-start | bytes 4915208 | tf_op jit(solution)/shard_map/ppermute | solution.py:249
  125.0 1.2 copy-start.11
  151.1 13.6 %copy-start.9 = (bf16[2560,640]{1,0:T(8,128)(2,1)S(1)}, bf16[2560,640]{1,0:T(8,128)(2,1)}, u32[]{:S(2)}) copy-start(bf16[2560,640]{1,0:T(8,128)(2,1)} %refs_0_.2) | copy-start | bytes 9830404
  164.7 2.1 copy-start.8
  169.1 52.2 %all-to-all-start.2 = ((bf16[8,64,1920]{2,1,0:T(8,128)(2,1)}), bf16[8,64,1920]{2,1,0:T(8,128)(2,1)S(1)}, u32[]{:S(2)}, u32[]{:S(2)}) async-start(bf16[8,64,1920]{2,1,0:T(8,128)(2,1)} %broadcast_in_dim.24), calls=%async_computation.2 | async-start | bytes 3932160 | tf_op jit(solution)/shard_map/all_to_all | solution.py:269
  237.2 14.0 %copy-start.14 = (f32[5,513]{1,0:T(8,128)S(1)}, f32[5,513]{1,0:T(8,128)}, u32[]{:S(2)}) copy-start(f32[5,513]{1,0:T(8,128)} %param.12) | copy-start | bytes 30784
  237.2 42.2 %all-to-all-start.3 = ((f32[8,64,768]{2,1,0:T(8,128)}), f32[8,64,768]{2,1,0:T(8,128)S(1)}, u32[]{:S(2)}, u32[]{:S(2)}) async-start(f32[8,64,768]{2,1,0:T(8,128)} %bitcast.81), calls=%async_computation.3 | async-start | bytes 3145728 | tf_op jit(solution)/shard_map/all_to_all | solution.py:281
  243.4 58.4 %collective-permute-start = (bf16[256,640]{1,0:T(8,128)(2,1)}, bf16[256,640]{1,0:T(8,128)(2,1)}, u32[]{:S(2)}, u32[]{:S(2)}) collective-permute-start(bf16[256,640]{1,0:T(8,128)(2,1)} %get-tuple-element.15), channel_id=1, source_target_pairs={{0,1},{1,2},{2,3},{3,4},{4,5},{5,6},{6,7},{8,9},{9,10},{10,11},{11... | collective-permute-start | bytes 983048 | tf_op jit(solution)/shard_map/ppermute | solution.py:262
  248.9 52.9 %collective-permute-start.1 = (bf16[256,640]{1,0:T(8,128)(2,1)}, bf16[256,640]{1,0:T(8,128)(2,1)}, u32[]{:S(2)}, u32[]{:S(2)}) collective-permute-start(bf16[256,640]{1,0:T(8,128)(2,1)} %get-tuple-element.13), channel_id=1, source_target_pairs={{0,1},{1,2},{2,3},{3,4},{4,5},{5,6},{6,7},{8,9},{9,10},{10,11},{11... | collective-permute-start | bytes 983048 | tf_op jit(solution)/shard_map/ppermute | solution.py:263
  285.5 68.7 %all-to-all-start.4 = ((bf16[32,64,640]{2,1,0:T(8,128)(2,1)}), bf16[32,64,640]{2,1,0:T(8,128)(2,1)S(1)}, u32[]{:S(2)}, u32[]{:S(2)}) async-start(bf16[32,64,640]{2,1,0:T(8,128)(2,1)} %broadcast_in_dim.25), calls=%async_computation.4 | async-start | bytes 5242880 | tf_op jit(solution)/shard_map/all_to_all | solution.py:269
  289.3 376.3 %all-gather.12.cloned.1.call-start = ((), (), s32[]{:S(2)}) async-start(), calls=%async_computation.8 | async-start | bytes 6553600 | tf_op jit(solution)/shard_map/all_gather | solution.py:333
  329.6 5.8 copy-start.16
  331.0 11.2 %collective-permute-start.4 = (bf16[256,640]{1,0:T(8,128)(2,1)S(1)}, bf16[256,640]{1,0:T(8,128)(2,1)S(1)}, u32[]{:S(2)}, u32[]{:S(2)}) collective-permute-start(bf16[256,640]{1,0:T(8,128)(2,1)S(1)} %get-tuple-element.25), channel_id=1, source_target_pairs={{0,24},{8,0},{16,8},{24,16},{1,25},{9,1},{17,9},{25,17},{2,26},{10... | collective-permute-start | bytes 983048 | tf_op jit(solution)/shard_map/ppermute | solution.py:303
  333.9 10.8 %collective-permute-start.3 = (bf16[256,640]{1,0:T(8,128)(2,1)S(1)}, bf16[256,640]{1,0:T(8,128)(2,1)S(1)}, u32[]{:S(2)}, u32[]{:S(2)}) collective-permute-start(bf16[256,640]{1,0:T(8,128)(2,1)S(1)} %get-tuple-element.26), channel_id=1, source_target_pairs={{0,16},{8,24},{16,0},{24,8},{1,17},{9,25},{17,1},{25,9},{2,18},{10... | collective-permute-start | bytes 983048 | tf_op jit(solution)/shard_map/ppermute | solution.py:303
  334.3 18.7 %collective-permute-start.2 = (bf16[256,640]{1,0:T(8,128)(2,1)S(1)}, bf16[256,640]{1,0:T(8,128)(2,1)S(1)}, u32[]{:S(2)}, u32[]{:S(2)}) collective-permute-start(bf16[256,640]{1,0:T(8,128)(2,1)S(1)} %get-tuple-element.27), channel_id=1, source_target_pairs={{0,8},{8,16},{16,24},{24,0},{1,9},{9,17},{17,25},{25,1},{2,10},{10... | collective-permute-start | bytes 983048 | tf_op jit(solution)/shard_map/ppermute | solution.py:303
  356.9 10.7 %copy-start.12 = (bf16[256,640]{1,0:T(8,128)(2,1)S(1)}, bf16[256,640]{1,0:T(8,128)(2,1)}, u32[]{:S(2)}) copy-start(bf16[256,640]{1,0:T(8,128)(2,1)} %get-tuple-element.16) | copy-start | bytes 983044
  356.9 13.1 %copy-start.13 = (bf16[256,640]{1,0:T(8,128)(2,1)S(1)}, bf16[256,640]{1,0:T(8,128)(2,1)}, u32[]{:S(2)}) copy-start(bf16[256,640]{1,0:T(8,128)(2,1)} %get-tuple-element.14) | copy-start | bytes 983044
  367.5 47.1 %copy-start.2 = (bf16[256,2560]{1,0:T(8,128)(2,1)}, bf16[256,2560]{1,0:T(8,128)(2,1)S(1)}, u32[]{:S(2)}) copy-start(bf16[256,2560]{1,0:T(8,128)(2,1)S(1)} %fusion.1.x_ref) | copy-start | bytes 3932164
  367.5 31.1 %collective-permute-start.7 = (bf16[256,2560]{1,0:T(8,128)(2,1)S(1)}, bf16[256,2560]{1,0:T(8,128)(2,1)S(1)}, u32[]{:S(2)}, u32[]{:S(2)}) collective-permute-start(bf16[256,2560]{1,0:T(8,128)(2,1)S(1)} %fusion.1.x_ref), channel_id=1, source_target_pairs={{0,8},{8,16},{16,24},{24,0},{1,9},{9,17},{17,25},{25,1},{2,10},{10... | collective-permute-start | bytes 3932168 | tf_op jit(solution)/shard_map/ppermute | solution.py:322
  367.6 62.7 %collective-permute-start.9 = (bf16[256,640]{1,0:T(8,128)(2,1)S(1)}, bf16[256,640]{1,0:T(8,128)(2,1)}, u32[]{:S(2)}, u32[]{:S(2)}) collective-permute-start(bf16[256,640]{1,0:T(8,128)(2,1)S(1)} %copy-done.12), channel_id=1, source_target_pairs={{1,0},{2,1},{3,2},{4,3},{5,4},{6,5},{7,6},{9,8},{10,9},{11,10},{12... | collective-permute-start | bytes 983048 | tf_op jit(solution)/shard_map/ppermute | solution.py:264
  370.1 60.3 %collective-permute-start.10 = (bf16[256,640]{1,0:T(8,128)(2,1)S(1)}, bf16[256,640]{1,0:T(8,128)(2,1)}, u32[]{:S(2)}, u32[]{:S(2)}) collective-permute-start(bf16[256,640]{1,0:T(8,128)(2,1)S(1)} %copy-done.13), channel_id=1, source_target_pairs={{1,0},{2,1},{3,2},{4,3},{5,4},{6,5},{7,6},{9,8},{10,9},{11,10},{12... | collective-permute-start | bytes 983048 | tf_op jit(solution)/shard_map/ppermute | solution.py:265
  398.6 1.1 copy-start.6
  430.2 63.3 %collective-permute-start.8 = (f32[256,2560]{1,0:T(8,128)}, f32[256,2560]{1,0:T(8,128)}, u32[]{:S(2)}, u32[]{:S(2)}) collective-permute-start(f32[256,2560]{1,0:T(8,128)} %shard_map.106), channel_id=1, source_target_pairs={{0,24},{8,0},{16,8},{24,16},{1,25},{9,1},{17,9},{25,17},{2,26},{10... | collective-permute-start | bytes 7864328 | tf_op jit(solution)/shard_map/ppermute | solution.py:328
  459.4 38.4 %collective-permute-start.13 = (bf16[256,640]{1,0:T(8,128)(2,1)S(1)}, bf16[256,640]{1,0:T(8,128)(2,1)S(1)}, u32[]{:S(2)}, u32[]{:S(2)}) collective-permute-start(bf16[256,640]{1,0:T(8,128)(2,1)S(1)} %get-tuple-element.33), channel_id=1, source_target_pairs={{0,24},{8,0},{16,8},{24,16},{1,25},{9,1},{17,9},{25,17},{2,26},{10... | collective-permute-start | bytes 983048 | tf_op jit(solution)/shard_map/ppermute | solution.py:303
  459.5 38.3 %collective-permute-start.12 = (bf16[256,640]{1,0:T(8,128)(2,1)S(1)}, bf16[256,640]{1,0:T(8,128)(2,1)S(1)}, u32[]{:S(2)}, u32[]{:S(2)}) collective-permute-start(bf16[256,640]{1,0:T(8,128)(2,1)S(1)} %get-tuple-element.34), channel_id=1, source_target_pairs={{0,16},{8,24},{16,0},{24,8},{1,17},{9,25},{17,1},{25,9},{2,18},{10... | collective-permute-start | bytes 983048 | tf_op jit(solution)/shard_map/ppermute | solution.py:303
  462.7 35.2 %collective-permute-start.11 = (bf16[256,640]{1,0:T(8,128)(2,1)S(1)}, bf16[256,640]{1,0:T(8,128)(2,1)}, u32[]{:S(2)}, u32[]{:S(2)}) collective-permute-start(bf16[256,640]{1,0:T(8,128)(2,1)S(1)} %get-tuple-element.35), channel_id=1, source_target_pairs={{0,8},{8,16},{16,24},{24,0},{1,9},{9,17},{17,25},{25,1},{2,10},{10... | collective-permute-start | bytes 983048 | tf_op jit(solution)/shard_map/ppermute | solution.py:303
  477.7 15.7 %copy-start.3 = (bf16[256,2560]{1,0:T(8,128)(2,1)S(1)}, bf16[256,2560]{1,0:T(8,128)(2,1)}, u32[]{:S(2)}) copy-start(bf16[256,2560]{1,0:T(8,128)(2,1)} %copy-done.2) | copy-start | bytes 3932164
  497.7 225.5 %all-gather.14.cloned.1.call-start = ((), (), s32[]{:S(2)}) async-start(), calls=%async_computation.9 | async-start | bytes 6553600 | tf_op jit(solution)/shard_map/all_gather | solution.py:333
  497.8 1.3 copy-start.17
  509.3 78.7 %copy-start.4 = (bf16[256,2560]{1,0:T(8,128)(2,1)}, bf16[256,2560]{1,0:T(8,128)(2,1)S(1)}, u32[]{:S(2)}) copy-start(bf16[256,2560]{1,0:T(8,128)(2,1)S(1)} %fusion.2.x_ref) | copy-start | bytes 3932164
  509.3 62.8 %collective-permute-start.14 = (bf16[256,2560]{1,0:T(8,128)(2,1)S(1)}, bf16[256,2560]{1,0:T(8,128)(2,1)S(1)}, u32[]{:S(2)}, u32[]{:S(2)}) collective-permute-start(bf16[256,2560]{1,0:T(8,128)(2,1)S(1)} %fusion.2.x_ref), channel_id=1, source_target_pairs={{0,24},{8,0},{16,8},{24,16},{1,25},{9,1},{17,9},{25,17},{2,26},{10... | collective-permute-start | bytes 3932168 | tf_op jit(solution)/shard_map/ppermute | solution.py:322
  572.1 1.1 copy-start.7
  603.6 57.7 %collective-permute-start.15 = (f32[256,2560]{1,0:T(8,128)}, f32[256,2560]{1,0:T(8,128)}, u32[]{:S(2)}, u32[]{:S(2)}) collective-permute-start(f32[256,2560]{1,0:T(8,128)} %shard_map.111), channel_id=1, source_target_pairs={{0,8},{8,16},{16,24},{24,0},{1,9},{9,17},{17,25},{25,1},{2,10},{10... | collective-permute-start | bytes 7864328 | tf_op jit(solution)/shard_map/ppermute | solution.py:328
  618.4 42.9 %copy-start.5 = (bf16[256,2560]{1,0:T(8,128)(2,1)S(1)}, bf16[256,2560]{1,0:T(8,128)(2,1)}, u32[]{:S(2)}) copy-start(bf16[256,2560]{1,0:T(8,128)(2,1)} %copy-done.4) | copy-start | bytes 3932164
  723.3 9.9 %copy-start.1 = (bf16[640,2560]{1,0:T(8,128)(2,1)S(1)}, bf16[640,2560]{1,0:T(8,128)(2,1)}, u32[]{:S(2)}) copy-start(bf16[640,2560]{1,0:T(8,128)(2,1)} %param.17) | copy-start | bytes 9830404
Sparse Core Ops, SparseCore 0:
  9.4 115.3 all-gather.5
  126.4 96.2 all-gather.9
  224.3 105.5 all-gather.7
  497.9 84.7 all-gather.11
  665.6 57.5 all-gather.13

commit v4 on v3

--- a/solution.py
+++ b/solution.py
@@ -89,32 +89,32 @@
 
 
 def _local_kernel(
-    half, window, seq_len, scale, n_heads, start_ref, q_ref, k_ref, v_ref, kh_ref, vh_ref,
+    half, window, seq_len, scale, n_heads, start_ref, q_ref, k_ref, v_ref, kl_ref, kr_ref, vl_ref, vr_ref,
     gk_ref, gv_ref, rb_ref, gpos_ref, o_ref, k_ext, v_ext, bias_ref,
 ):
-    blk = pl.program_id(0)
+    step = pl.program_id(0)
+    blk = 2 * step + half
     span = 3 * window
     rows_all = k_ref.shape[0]
-    held = k_ext.shape[0] - window
     hd = q_ref.shape[1] // n_heads
 
-    @pl.when(blk == 0)
+    @pl.when(step == 0)
     def _():
-        for ext, mid, halo in ((k_ext, k_ref, kh_ref), (v_ext, v_ref, vh_ref)):
-            if half == 0:
-                ext[:window] = halo[...]
-                ext[window:] = mid[:held]
-            else:
-                ext[:held] = mid[rows_all - held:]
-                ext[held:] = halo[...]
-        row = lax.broadcasted_iota(jnp.int32, (window, span), 0)
+        for ext, left, mid, right in ((k_ext, kl_ref, k_ref, kr_ref), (v_ext, vl_ref, v_ref, vr_ref)):
+            ext[:window] = left[...]
+            ext[window:window + rows_all] = mid[...]
+            ext[window + rows_all:] = right[...]
+        group = 8
+        row = lax.broadcasted_iota(jnp.int32, (group, span), 0)
         for h in range(n_heads):
-            bias = jnp.broadcast_to(rb_ref[h], (window, span))
-            for bit in range(window.bit_length() - 1):
+            bias = jnp.broadcast_to(rb_ref[h], (group, span))
+            for bit in range(group.bit_length() - 1):
                 bias = jnp.where(((row >> bit) & 1) == 1, pltpu.roll(bias, 1 << bit, 1), bias)
-            bias_ref[h] = bias
-
-    first = start_ref[0] + half * (rows_all // 2) + blk * window
+            bias_ref[h, :group] = bias
+            for g in range(1, window // group):
+                bias_ref[h, g * group:(g + 1) * group] = pltpu.roll(bias, g * group, 1)
+
+    first = start_ref[0] + blk * window
     key_pos = first - window + lax.broadcasted_iota(jnp.int32, (1, span), 1)
     edge = jnp.where((key_pos >= 0) & (key_pos < seq_len), 0.0, NEG_INF).astype(F32)
     dist = first + lax.broadcasted_iota(jnp.int32, (window, 1), 0) - gpos_ref[...]
@@ -134,21 +134,21 @@
         o_ref[:, cols] = out.astype(BF16)
 
 
-def _local_attn(half, row_start, q, k, v, k_halo, v_halo, glob_k, glob_v, bias_rows, glob_pos, window, seq_len, scale):
-    rows, width = q.shape[0] // 2, q.shape[1]
+def _local_attn(half, row_start, q, k, v, halos, glob_k, glob_v, bias_rows, glob_pos, window, seq_len, scale):
+    rows, width = q.shape
     n_heads = bias_rows.shape[0]
     n_glob = glob_k.shape[0]
     span = 3 * window
-    n_blk = rows // window
+    n_blk = rows // (2 * window)
 
     def whole(array):
         return pl.BlockSpec(array.shape, lambda c, s: (0,) * array.ndim, pipeline_mode=pl.Buffered(1))
 
-    held = (k, v, k_halo, v_halo, glob_k, glob_v, bias_rows, glob_pos[None, :])
+    held = (k, v, *halos, glob_k, glob_v, bias_rows, glob_pos[None, :])
     grid_spec = pltpu.PrefetchScalarGridSpec(
         num_scalar_prefetch=1,
         grid=(n_blk,),
-        in_specs=[pl.BlockSpec((window, width), lambda c, s: (c + half * n_blk, 0))] + [whole(array) for array in held],
+        in_specs=[pl.BlockSpec((window, width), lambda c, s: (2 * c + half, 0))] + [whole(array) for array in held],
         out_specs=pl.BlockSpec((window, width), lambda c, s: (c, 0)),
         scratch_shapes=[
             pltpu.VMEM((rows + 2 * window, width), BF16),
@@ -159,11 +159,11 @@
     return pl.pallas_call(
         functools.partial(_local_kernel, half, window, seq_len, scale * LOG2E, n_heads),
         grid_spec=grid_spec,
-        out_shape=jax.ShapeDtypeStruct((rows, width), BF16),
+        out_shape=jax.ShapeDtypeStruct((rows // 2, width), BF16),
         cost_estimate=pl.CostEstimate(
-            flops=16 * rows * (span + n_glob) * width,
-            bytes_accessed=2 * (2 * rows * width + 2 * (rows + 2 * window + n_glob) * width),
-            transcendentals=n_heads * rows * (span + n_glob),
+            flops=8 * rows * (span + n_glob) * width,
+            bytes_accessed=2 * (rows * width + 2 * (rows + 2 * window + n_glob) * width),
+            transcendentals=n_heads * rows * (span + n_glob) // 2,
         ),
     )(row_start[None], q, *held)
 
@@ -259,10 +259,9 @@
 
         k, v = _project(tokens, w_key, w_value)
         (q,) = _project(tokens, w_query)
-        k_left = lax.ppermute(k[local_rows - window:], "sp", to_right)
-        v_left = lax.ppermute(v[local_rows - window:], "sp", to_right)
-        k_right = lax.ppermute(k[:window], "sp", to_left)
-        v_right = lax.ppermute(v[:window], "sp", to_left)
+        halos = []
+        for rows, route in ((k[local_rows - window:], to_right), (k[:window], to_left), (v[local_rows - window:], to_right), (v[:window], to_left)):
+            halos.append(lax.ppermute(rows, "sp", route))
 
         def to_all(block, axes, size):
             copies = jnp.broadcast_to(block[None], (size,) + block.shape)
@@ -271,11 +270,11 @@
         glob_rows = glob_rows.reshape(n_seq, glob_blk, share).astype(F32).sum(axis=0).astype(BF16)
         glob_rows = to_all(glob_rows, "tp", n_tp)
         glob_rows = glob_rows.transpose(1, 0, 2).reshape(glob_blk, model_dim)
-        glob_qkv = jnp.concatenate([_dot(glob_rows, w).astype(BF16) for w in (w_query_glob, w_key, w_value)], axis=1)
-        glob_qkv = to_all(glob_qkv, "sp", n_seq).reshape(n_glob, 3 * width)
-        glob_q = glob_qkv[:, :width]
-        glob_k = glob_qkv[:, width:2 * width]
-        glob_v = glob_qkv[:, 2 * width:]
+        glob_q = to_all(_dot(glob_rows, w_query_glob).astype(BF16), "sp", n_seq).reshape(n_glob, width)
+        glob_kv = jnp.concatenate([_dot(glob_rows, w).astype(BF16) for w in (w_key, w_value)], axis=1)
+        glob_kv = to_all(glob_kv, "sp", n_seq).reshape(n_glob, 2 * width)
+        glob_k = glob_kv[:, :width]
+        glob_v = glob_kv[:, width:]
 
         parts = _glob_partial(glob_q, k, v, n_heads, scale)
         parts = lax.all_to_all(parts, "sp", 0, 0, tiled=True).reshape(n_seq, glob_blk, parts.shape[1])
@@ -290,11 +289,11 @@
         pad = jnp.full((n_heads, 3 * window - rel_width), NEG_INF, F32)
         bias_rows = jnp.concatenate([rel_bias * LOG2E, pad], axis=1)[:, None, :]
         blk = local_rows // (2 * n_tp)
-        own_tokens = lax.dynamic_index_in_dim(tokens.reshape(2, n_tp, blk, model_dim), tp_index, 1, keepdims=False)
-        hidden = []
-        for half, (k_halo, v_halo) in enumerate(((k_left, v_left), (k_right, v_right))):
+        assert blk == window
+        rows_held = []
+        for half in range(2):
             win_out = _local_attn(
-                half, row_start, q, k, v, k_halo, v_halo, glob_k, glob_v, bias_rows, glob_pos, window, seq_len, scale
+                half, row_start, q, k, v, halos, glob_k, glob_v, bias_rows, glob_pos, window, seq_len, scale
             )
             win_out = win_out.reshape(n_tp, blk, width)
             held = [lax.dynamic_index_in_dim(win_out, tp_index, 0, keepdims=False)]
@@ -302,36 +301,34 @@
                 sent = lax.dynamic_index_in_dim(win_out, lax.rem(tp_index + shift, n_tp), 0, keepdims=False)
                 held.append(lax.ppermute(sent, "tp", [(i, (i + shift) % n_tp) for i in range(n_tp)]))
             held = jnp.stack(held)
-            win_out = jnp.concatenate(
-                [
-                    lax.dynamic_index_in_dim(held, lax.rem(tp_index - source + n_tp, n_tp), 0, keepdims=False)
-                    for source in range(n_tp)
-                ],
-                axis=1,
+            rows_held.append(
+                jnp.concatenate(
+                    [
+                        lax.dynamic_index_in_dim(held, lax.rem(tp_index - source + n_tp, n_tp), 0, keepdims=False)
+                        for source in range(n_tp)
+                    ],
+                    axis=1,
+                )
             )
-            first = row_start + half * (local_rows // 2) + tp_index * blk
-            put = (first + jnp.arange(blk, dtype=jnp.int32))[:, None] == glob_pos[None, :]
-            attn_rows = jnp.where(
-                put.any(axis=1, keepdims=True), _dot(put.astype(BF16), glob_out).astype(BF16), win_out
-            )
-            hidden.append((own_tokens[half].astype(F32) + _dot(attn_rows, out_full)).astype(BF16))
-
-        there, home = (to_next, to_prev), (to_prev, to_next)
-        guests = []
-        for half in range(2):
-            guests.append(lax.ppermute(hidden[half], "tp", there[half]))
-        own_part = [_mlp(hidden[half], w_up, w_down) for half in range(2)]
-        back = []
-        for half in range(2):
-            guest_part = _mlp(guests[half], w_up, w_down)
-            guest_part = _mlp(guests[half], up_twin, down_twin, guest_part)
-            back.append(lax.ppermute(guest_part, "tp", home[half]))
-        outs = []
-        for half in range(2):
-            part = _mlp(hidden[half], up_twin, down_twin, own_part[half])
-            out = (hidden[half].astype(F32) + (part + back[half])).astype(BF16)
-            outs.append(lax.all_gather(out, "tp", axis=0, tiled=True))
-        return jnp.concatenate(outs, axis=0)
+        rows_held = jnp.concatenate(rows_held, axis=0)
+        own_first = tp_index * 2 * blk
+        put = (row_start + own_first + jnp.arange(2 * blk, dtype=jnp.int32))[:, None] == glob_pos[None, :]
+        attn_rows = jnp.where(put.any(axis=1, keepdims=True), _dot(put.astype(BF16), glob_out).astype(BF16), rows_held)
+        own_tokens = lax.dynamic_slice_in_dim(tokens, own_first, 2 * blk, 0)
+        hidden = (own_tokens.astype(F32) + _dot(attn_rows, out_full)).astype(BF16)
+
+        guest_0 = lax.ppermute(hidden[:blk], "tp", to_next)
+        guest_1 = lax.ppermute(hidden[blk:], "tp", to_prev)
+        own_part = _mlp(hidden, w_up, w_down)
+        guests = jnp.concatenate([guest_0, guest_1], axis=0)
+        guest_part = _mlp(guests, w_up, w_down)
+        guest_part = _mlp(guests, up_twin, down_twin, guest_part)
+        back_0 = lax.ppermute(guest_part[:blk], "tp", to_prev)
+        back_1 = lax.ppermute(guest_part[blk:], "tp", to_next)
+        own_part = _mlp(hidden, up_twin, down_twin, own_part)
+        part = own_part + jnp.concatenate([back_0, back_1], axis=0)
+        out = (hidden.astype(F32) + part).astype(BF16)
+        return lax.all_gather(out, "tp", axis=0, tiled=True)
 
     row_spec = P(("batch", "sp"), None)
     col_spec = P(None, "tp")

time: 749 us -> 657 us (0.88)
  waiting for transfers between devices: 341 us -> 287 us
  Pallas kernels: 226 us -> 183 us
  local copies, waits for them, and re-layouts: 31.8 us -> 49.9 us
  starting transfers between devices: 47.1 us -> 58.4 us
  blocking collectives: 31.9 us -> 21 us
  other arithmetic: 20.3 us -> 10.4 us
    ppermute x8, waiting for transfers between devices: 110 us -> 39.9 us  [the longest x1 27.4 us: layer(): guest_0 = lax.ppermute(hidden[:blk], 'tp', to_next)]
    all_gather x2 -> x1, waiting for transfers between devices: 57.8 us -> 99.5 us  [layer(): return lax.all_gather(out, 'tp', axis=0, tiled=True)]
    pallas_call x8 -> x4, Pallas kernels: 122 us -> 90.2 us  [_mlp(): pl.pallas_call(functools.partial(_mlp_kernel, n_steps), grid=(n_steps + 1...]
    ppermute x1, waiting for transfers between devices: 42.2 us -> 61.3 us  [layer(): down_piece = lax.ppermute(piece(w_down), 'tp', to_twin)]
    ppermute x1, waiting for transfers between devices: 61.3 us -> 42.2 us  [layer(): up_piece = lax.ppermute(piece(w_up), 'tp', to_twin)]
    pallas_call x2, Pallas kernels: 55.4 us -> 43.3 us  [_local_attn(): pl.pallas_call(functools.partial(_local_kernel, half, window, seq_len, sc...]
    all_to_all x1, waiting for transfers between devices: 27.6 us -> 16.5 us  [layer(): lax.all_to_all(parts, 'sp', 0, 0, tiled=True)]
    all_to_all x1 -> x0, blocking collectives: 10.9 us -> none  [to_all(): return lax.all_to_all(copies, axes, 0, 0, tiled=True)]
  transfers between devices with their start and end apart: 24 -> 25, of which waited for: 11 -> 12; matrix products, arithmetic and copies ran while one was open for 8% -> 9% of each run, Pallas kernels for 30% -> 25%
where the time goes in v4:
time: 657 us; the launch traced here: 648 us
  waiting for transfers between devices  287 us (44%)
  Pallas kernels  183 us (28%)
  starting transfers between devices  58.4 us (9%)
  local copies, waits for them, and re-layouts  49.9 us (8%)
  matrix products  25.3 us (4%)
  blocking collectives  21 us (3%)
  between operations  13.7 us (2%)
  other arithmetic  10.4 us (2%)
    all_gather x1, waiting for transfers between devices, layer(): return lax.all_gather(out, 'tp', axis=0, tiled=True)  99.5 us
    pallas_call x4, Pallas kernels, _mlp(): pl.pallas_call(functools.partial(_mlp_kernel, n_steps), grid=(n_steps + 1...  90.2 us
    ppermute x1, waiting for transfers between devices, layer(): down_piece = lax.ppermute(piece(w_down), 'tp', to_twin)  61.3 us
    pallas_call x2, Pallas kernels, _local_attn(): pl.pallas_call(functools.partial(_local_kernel, half, window, seq_len, sc...  43.3 us
    ppermute x1, waiting for transfers between devices, layer(): up_piece = lax.ppermute(piece(w_up), 'tp', to_twin)  42.2 us
    pallas_call x2, Pallas kernels, _project(): pl.pallas_call(_proj_kernel, grid=(rows // blk,), in_specs=[pl.BlockSpec(...  34.1 us
    ppermute x1, waiting for transfers between devices, layer(): guest_0 = lax.ppermute(hidden[:blk], 'tp', to_next)  27.4 us
    dot_general x5, matrix products, _dot(): return jnp.dot(lhs, rhs, preferred_element_type=F32)  25.3 us
  transfers between devices with their start and end apart: 25, of which 12 were waited for; matrix products, arithmetic and copies ran while one was open for 9% of the time, Pallas kernels for 25%

profile of v4, /device:TPU:97, one launch (start us, length us, event | category | flops | bytes accessed | tf_op | source)
XLA Modules:
  0.0 648.3 jit_solution(4523562928226331117)
XLA Ops:
  6.6 1.9 copy-done
  10.9 4.9 collective-permute-start.10
  15.9 42.2 %collective-permute-done.10 = bf16[320,2560]{1,0:T(8,128)(2,1)S(1)} collective-permute-done((bf16[320,2560]{1,0:T(8,128)(2,1)S(1)}, bf16[320,2560]{1,0:T(8,128)(2,1)S(1)}, u32[]{:S(2)}, u32[]{:S(2)}) %collective-permute-start.10) | collective-permute-done | bytes 1638432 | tf_op jit(solution)/shard_map/ppermute | solution.py:249
  60.9 2.8 collective-permute-start.11
  63.7 61.3 %collective-permute-done.11 = bf16[320,2560]{1,0:T(8,128)(2,1)S(1)} collective-permute-done((bf16[320,2560]{1,0:T(8,128)(2,1)S(1)}, bf16[320,2560]{1,0:T(8,128)(2,1)S(1)}, u32[]{:S(2)}, u32[]{:S(2)}) %collective-permute-start.11) | collective-permute-done | bytes 1638432 | tf_op jit(solution)/shard_map/ppermute | solution.py:250
  126.3 3.7 fusion.6
  130.0 21.0 %all_to_all.38 = bf16[8,64,640]{2,1,0:T(8,128)(2,1)S(1)} all-to-all(bf16[8,64,640]{2,1,0:T(8,128)(2,1)S(1)} %bitcast.79), channel_id=1, replica_groups=mesh['batch'=1,'tp'=4,'sp'=8] {'sp'}, dimensions={0} | all-to-all | bytes 1310720 | tf_op jit(solution)/shard_map/all_to_all | solution.py:258
  151.9 4.9 all-to-all-start.1
  156.7 21.6 %shard_map.100 = (bf16[2048,640]{1,0:T(8,128)(2,1)}, bf16[2048,640]{1,0:T(8,128)(2,1)}) custom-call(bf16[2048,2560]{1,0:T(8,128)(2,1)} %x_ref.3, bf16[2560,640]{1,0:T(8,128)(2,1)} %refs_0_.2, bf16[2560,640]{1,0:T(8,128)(2,1)} %refs_1_.1), custom_call_target="tpu_custom_call" | custom-call | flops 13421772800 | bytes 22282240 | tf_op jit(solution)/shard_map/pallas_call | solution.py:40
  178.4 2.8 convolution_convert_fusion.3
  182.1 4.7 all-to-all-start.2
  186.8 2.9 convolution_convert_fusion.1
  190.6 14.6 %all-to-all-done.2 = bf16[8,64,640]{2,1,0:T(8,128)(2,1)S(1)} async-done(((bf16[8,64,640]{2,1,0:T(8,128)(2,1)}), bf16[8,64,640]{2,1,0:T(8,128)(2,1)S(1)}, u32[]{:S(2)}, u32[]{:S(2)}) %all-to-all-start.2) | async-done | bytes 655392 | tf_op jit(solution)/shard_map/all_to_all | solution.py:268
  206.4 4.3 all-to-all-start.5
  210.8 2.0 fusion.19
  212.7 3.6 collective-permute-start
  216.3 2.0 collective-permute-start.1
  218.3 15.4 %glob_attn.1 = f32[512,768]{1,0:T(8,128)} custom-call(bf16[512,640]{1,0:T(8,128)(2,1)} %bitcast.78, bf16[2048,640]{1,0:T(8,128)(2,1)} %get-tuple-element.7.k_ref, bf16[2048,640]{1,0:T(8,128)(2,1)} %get-tuple-element.8.v_ref), custom_call_target="tpu_custom_call" | custom-call | flops 10737418240 | bytes 7208960 | tf_op jit(solution)/shard_map/glob_attn/pallas_call | solution.py:76
  234.1 6.2 all-to-all-start.3
  240.3 2.0 fusion.18
  242.3 3.6 collective-permute-start.2
  245.9 2.1 collective-permute-start.3
  248.7 12.5 %shard_map.101.q_ref = bf16[2048,640]{1,0:T(8,128)(2,1)} custom-call(bf16[2048,2560]{1,0:T(8,128)(2,1)} %x_ref.3, bf16[2560,640]{1,0:T(8,128)(2,1)} %refs_0_.3), custom_call_target="tpu_custom_call" | custom-call | flops 6710886400 | bytes 16384000 | tf_op jit(solution)/shard_map/pallas_call | solution.py:40
  262.4 16.5 %all-to-all-done.3 = f32[8,64,768]{2,1,0:T(8,128)S(1)} async-done(((f32[8,64,768]{2,1,0:T(8,128)}), f32[8,64,768]{2,1,0:T(8,128)S(1)}, u32[]{:S(2)}, u32[]{:S(2)}) %all-to-all-start.3) | async-done | bytes 1572896 | tf_op jit(solution)/shard_map/all_to_all | solution.py:280
  279.1 1.9 mul.40
  285.0 5.3 all-to-all-start.4
  290.5 21.7 %shard_map.102 = bf16[1024,640]{1,0:T(8,128)(2,1)} custom-call(s32[1]{0:T(128)} %bitcast.7.start_ref, bf16[2048,640]{1,0:T(8,128)(2,1)} %shard_map.101.q_ref, bf16[2048,640]{1,0:T(8,128)(2,1)} %get-tuple-element.7.k_ref, bf16[2048,640]{1,0:T(8,128)(2,1)} %get-tuple-element.8.v_ref, bf16[256,640]{1,0:T(8,128)(2,1)} %collective-permute-done.kl_ref, ...), custom_call_target="tpu_custom_call" | custom-call | flops 13421772800 | bytes 10485760 | tf_op jit(solution)/shard_map/pallas_call | solution.py:159
  312.2 2.2 constant_dynamic-slice_fusion.4
  315.8 2.6 collective-permute-start.5
  319.6 21.6 %shard_map.103 = bf16[1024,640]{1,0:T(8,128)(2,1)} custom-call(s32[1]{0:T(128)} %bitcast.7.start_ref, bf16[2048,640]{1,0:T(8,128)(2,1)} %shard_map.101.q_ref, bf16[2048,640]{1,0:T(8,128)(2,1)} %get-tuple-element.7.k_ref, bf16[2048,640]{1,0:T(8,128)(2,1)} %get-tuple-element.8.v_ref, bf16[256,640]{1,0:T(8,128)(2,1)} %collective-permute-done.kl_ref, ...), custom_call_target="tpu_custom_call" | custom-call | flops 13421772800 | bytes 10485760 | tf_op jit(solution)/shard_map/pallas_call | solution.py:159
  341.2 2.3 constant_dynamic-slice_fusion.3
  348.9 5.2 collective-permute-done.7
  354.1 4.8 collective-permute-done.8
  358.9 2.0 collective-permute-done.9
  363.4 2.6 copy.15
  366.0 15.2 %add_convert_fusion.x_ref = bf16[512,2560]{1,0:T(8,128)(2,1)S(1)} fusion(bf16[2560,2560]{1,0:T(8,128)(2,1)} %all-gather.5.cloned.1.call-done, bf16[2048,2560]{1,0:T(8,128)(2,1)} %x_ref.3, s32[]{:T(128)S(6)} %select_n.44, bf16[512,2560]{0,1:T(8,128)(2,1)} %bitcast.72, bf16[256,640]{1,0:T(8,128)(2,1)} %get-tuple-element.28, ...), kind=kOutput, calls=%fused_computation.3 | convolution fusion | flops 8080850944 | bytes 23597572 | tf_op jit(solution)/shard_map/dot_general | solution.py:19
  384.1 2.4 collective-permute-start.13
  386.5 27.4 %collective-permute-done.12 = bf16[256,2560]{1,0:T(8,128)(2,1)S(1)} collective-permute-done((bf16[256,2560]{1,0:T(8,128)(2,1)S(1)}, bf16[256,2560]{1,0:T(8,128)(2,1)S(1)}, u32[]{:S(2)}, u32[]{:S(2)}) %collective-permute-start.12) | collective-permute-done | bytes 1310752 | tf_op jit(solution)/shard_map/ppermute | solution.py:320
  416.2 21.8 %shard_map.106.refs_0_ = f32[512,2560]{1,0:T(8,128)} custom-call(bf16[512,2560]{1,0:T(8,128)(2,1)} %constant_dynamic-update-slice_fusion.x_ref, bf16[2560,2560]{1,0:T(8,128)(2,1)} %up_ref.3, bf16[2560,2560]{1,0:T(8,128)(2,1)} %down_ref.3), custom_call_target="tpu_custom_call" | custom-call | flops 13421772800 | bytes 34078720 | tf_op jit(solution)/shard_map/pallas_call | solution.py:200
  438.0 23.2 %shard_map.107 = f32[512,2560]{1,0:T(8,128)} custom-call(bf16[512,2560]{1,0:T(8,128)(2,1)} %constant_dynamic-update-slice_fusion.x_ref, bf16[2560,2560]{1,0:T(8,128)(2,1)} %all-gather.7.cloned.1.call-done.up_ref, bf16[2560,2560]{1,0:T(8,128)(2,1)} %all-gather.9.cloned.1.call-done.down_ref, f32[512,2560]{1,0:T(8,128)} %shard_map.106.refs_0_), custom_call_target="tpu_custom_call" | custom-call | flops 13421772800 | bytes 34078720 | tf_op jit(solution)/shard_map/pallas_call | solution.py:200
  461.2 5.2 fusion.16
  468.5 21.8 %shard_map.104.refs_0_ = f32[512,2560]{1,0:T(8,128)} custom-call(bf16[512,2560]{1,0:T(8,128)(2,1)} %copy-done.2, bf16[2560,2560]{1,0:T(8,128)(2,1)} %up_ref.3, bf16[2560,2560]{1,0:T(8,128)(2,1)} %down_ref.3), custom_call_target="tpu_custom_call" | custom-call | flops 13421772800 | bytes 34078720 | tf_op jit(solution)/shard_map/pallas_call | solution.py:200
  490.3 23.4 %shard_map.105 = f32[512,2560]{1,0:T(8,128)} custom-call(bf16[512,2560]{1,0:T(8,128)(2,1)} %copy-done.2, bf16[2560,2560]{1,0:T(8,128)(2,1)} %all-gather.7.cloned.1.call-done.up_ref, bf16[2560,2560]{1,0:T(8,128)(2,1)} %all-gather.9.cloned.1.call-done.down_ref, f32[512,2560]{1,0:T(8,128)} %shard_map.104.refs_0_), custom_call_target="tpu_custom_call" | custom-call | flops 13421772800 | bytes 34078720 | tf_op jit(solution)/shard_map/pallas_call | solution.py:200
  513.7 9.5 %collective-permute-done.14 = f32[256,2560]{1,0:T(8,128)} collective-permute-done((f32[256,2560]{1,0:T(8,128)}, f32[256,2560]{1,0:T(8,128)}, u32[]{:S(2)}, u32[]{:S(2)}) %collective-permute-start.14) | collective-permute-done | bytes 2621472 | tf_op jit(solution)/shard_map/ppermute | solution.py:326
  523.2 3.0 collective-permute-done.15
  526.2 6.9 %fusion.1 = bf16[512,2560]{1,0:T(8,128)(2,1)} fusion(f32[512,2560]{1,0:T(8,128)} %shard_map.105, f32[256,2560]{1,0:T(8,128)} %collective-permute-done.15, f32[256,2560]{1,0:T(8,128)} %collective-permute-done.14, bf16[512,2560]{1,0:T(8,128)(2,1)S(1)} %copy-done.3), kind=kLoop, calls=%fused_computation.2 | loop fusion | flops 6553600 | bytes 15728640 | tf_op jit(solution)/shard_map/convert_element_type | solution.py:330
  533.2 99.5 %all-gather.11.cloned.1.call-done = bf16[2048,2560]{1,0:T(8,128)(2,1)} async-done(((bf16[512,2560]{1,0:T(8,128)(2,1)}), bf16[2048,2560]{1,0:T(8,128)(2,1)}) %all-gather.11.cloned.1.call-update) | async-done | bytes 10485776 | tf_op jit(solution)/shard_map/all_gather | solution.py:331
  632.7 8.9 %copy.21 = bf16[2048,2560]{1,0:T(8,128)(2,1)} copy(bf16[2048,2560]{1,0:T(8,128)(2,1)} %all-gather.11.cloned.1.call-done) | data formatting | bytes 20971520
  (84 shorter events, 34.9 us)
Async XLA Ops:
  6.5 1.9 copy-start
  6.6 359.5 %all-gather.5.cloned.1.call-start = ((), (), s32[]{:S(2)}) async-start(), calls=%async_computation.6 | async-start | bytes 13516800 | tf_op jit(solution)/shard_map/all_gather | solution.py:248
  9.3 428.6 %all-gather.7.cloned.1.call-start = ((), (), s32[]{:S(2)}) async-start(), calls=%async_computation.7 | async-start | bytes 14745600 | tf_op jit(solution)/shard_map/all_gather | solution.py:251
  10.9 47.1 %collective-permute-start.10 = (bf16[320,2560]{1,0:T(8,128)(2,1)S(1)}, bf16[320,2560]{1,0:T(8,128)(2,1)S(1)}, u32[]{:S(2)}, u32[]{:S(2)}) collective-permute-start(bf16[320,2560]{1,0:T(8,128)(2,1)S(1)} %constant_dynamic-slice_fusion.1), channel_id=1, source_target_pairs={{0,16},{8,24},{16,0},{24,8},{1,17},{9,25},{17,1},{25,9},{2,18},{10... | collective-permute-start | bytes 4915208 | tf_op jit(solution)/shard_map/ppermute | solution.py:249
  58.0 1.2 copy-start.5
  59.3 67.0 %copy-start.10 = (s32[512]{0:T(512)S(1)}, s32[512]{0:T(512)}, u32[]{:S(2)}) copy-start(s32[512]{0:T(512)} %param.11) | copy-start | bytes 6148
  59.3 378.7 %all-gather.9.cloned.1.call-start = ((), (), s32[]{:S(2)}) async-start(), calls=%async_computation.8 | async-start | bytes 14745600 | tf_op jit(solution)/shard_map/all_gather | solution.py:252
  60.9 64.1 %collective-permute-start.11 = (bf16[320,2560]{1,0:T(8,128)(2,1)S(1)}, bf16[320,2560]{1,0:T(8,128)(2,1)S(1)}, u32[]{:S(2)}, u32[]{:S(2)}) collective-permute-start(bf16[320,2560]{1,0:T(8,128)(2,1)S(1)} %constant_dynamic-slice_fusion), channel_id=1, source_target_pairs={{0,16},{8,24},{16,0},{24,8},{1,17},{9,25},{17,1},{25,9},{2,18},{10... | collective-permute-start | bytes 4915208 | tf_op jit(solution)/shard_map/ppermute | solution.py:250
  125.0 1.2 copy-start.6
  151.9 26.5 %all-to-all-start.1 = ((bf16[4,64,640]{2,1,0:T(8,128)(2,1)}), bf16[4,64,640]{2,1,0:T(8,128)(2,1)S(1)}, u32[]{:S(2)}, u32[]{:S(2)}) async-start(bf16[4,64,640]{2,1,0:T(8,128)(2,1)} %broadcast_in_dim.20), calls=%async_computation.1 | async-start | bytes 655360 | tf_op jit(solution)/shard_map/all_to_all | solution.py:268
  182.1 23.1 %all-to-all-start.2 = ((bf16[8,64,640]{2,1,0:T(8,128)(2,1)}), bf16[8,64,640]{2,1,0:T(8,128)(2,1)S(1)}, u32[]{:S(2)}, u32[]{:S(2)}) async-start(bf16[8,64,640]{2,1,0:T(8,128)(2,1)} %broadcast_in_dim.21), calls=%async_computation.2 | async-start | bytes 1310720 | tf_op jit(solution)/shard_map/all_to_all | solution.py:268
  186.8 3.0 copy-start.4
  205.2 7.5 %copy-start.7 = (bf16[8,64,640]{2,1,0:T(8,128)(2,1)}, bf16[8,64,640]{2,1,0:T(8,128)(2,1)S(1)}, u32[]{:S(2)}) copy-start(bf16[8,64,640]{2,1,0:T(8,128)(2,1)S(1)} %all-to-all-done.2) | copy-start | bytes 1966084
  206.4 27.7 %all-to-all-start.5 = ((bf16[8,64,1280]{2,1,0:T(8,128)(2,1)}), bf16[8,64,1280]{2,1,0:T(8,128)(2,1)S(1)}, u32[]{:S(2)}, u32[]{:S(2)}) async-start(bf16[8,64,1280]{2,1,0:T(8,128)(2,1)} %broadcast_in_dim.24), calls=%async_computation.5 | async-start | bytes 2621440 | tf_op jit(solution)/shard_map/all_to_all | solution.py:268
  212.7 77.7 %collective-permute-start = (bf16[256,640]{1,0:T(8,128)(2,1)}, bf16[256,640]{1,0:T(8,128)(2,1)}, u32[]{:S(2)}, u32[]{:S(2)}) collective-permute-start(bf16[256,640]{1,0:T(8,128)(2,1)} %get-tuple-element.18), channel_id=1, source_target_pairs={{0,1},{1,2},{2,3},{3,4},{4,5},{5,6},{6,7},{8,9},{9,10},{10,11},{11... | collective-permute-start | bytes 983048 | tf_op jit(solution)/shard_map/ppermute | solution.py:264
  216.3 74.1 %collective-permute-start.1 = (bf16[256,640]{1,0:T(8,128)(2,1)}, bf16[256,640]{1,0:T(8,128)(2,1)}, u32[]{:S(2)}, u32[]{:S(2)}) collective-permute-start(bf16[256,640]{1,0:T(8,128)(2,1)} %get-tuple-element.17), channel_id=1, source_target_pairs={{1,0},{2,1},{3,2},{4,3},{5,4},{6,5},{7,6},{9,8},{10,9},{11,10},{12... | collective-permute-start | bytes 983048 | tf_op jit(solution)/shard_map/ppermute | solution.py:264
  233.7 14.4 %copy-start.9 = (f32[5,513]{1,0:T(8,128)S(1)}, f32[5,513]{1,0:T(8,128)}, u32[]{:S(2)}) copy-start(f32[5,513]{1,0:T(8,128)} %param.12) | copy-start | bytes 30784
  234.1 44.8 %all-to-all-start.3 = ((f32[8,64,768]{2,1,0:T(8,128)}), f32[8,64,768]{2,1,0:T(8,128)S(1)}, u32[]{:S(2)}, u32[]{:S(2)}) async-start(f32[8,64,768]{2,1,0:T(8,128)} %bitcast.73), calls=%async_computation.3 | async-start | bytes 3145728 | tf_op jit(solution)/shard_map/all_to_all | solution.py:280
  242.3 48.1 %collective-permute-start.2 = (bf16[256,640]{1,0:T(8,128)(2,1)}, bf16[256,640]{1,0:T(8,128)(2,1)}, u32[]{:S(2)}, u32[]{:S(2)}) collective-permute-start(bf16[256,640]{1,0:T(8,128)(2,1)} %get-tuple-element.16), channel_id=1, source_target_pairs={{0,1},{1,2},{2,3},{3,4},{4,5},{5,6},{6,7},{8,9},{9,10},{10,11},{11... | collective-permute-start | bytes 983048 | tf_op jit(solution)/shard_map/ppermute | solution.py:264
  245.9 44.5 %collective-permute-start.3 = (bf16[256,640]{1,0:T(8,128)(2,1)}, bf16[256,640]{1,0:T(8,128)(2,1)}, u32[]{:S(2)}, u32[]{:S(2)}) collective-permute-start(bf16[256,640]{1,0:T(8,128)(2,1)} %get-tuple-element.15), channel_id=1, source_target_pairs={{1,0},{2,1},{3,2},{4,3},{5,4},{6,5},{7,6},{9,8},{10,9},{11,10},{12... | collective-permute-start | bytes 983048 | tf_op jit(solution)/shard_map/ppermute | solution.py:264
  285.0 78.4 %all-to-all-start.4 = ((bf16[32,64,640]{2,1,0:T(8,128)(2,1)}), bf16[32,64,640]{2,1,0:T(8,128)(2,1)S(1)}, u32[]{:S(2)}, u32[]{:S(2)}) async-start(bf16[32,64,640]{2,1,0:T(8,128)(2,1)} %broadcast_in_dim.22), calls=%async_computation.4 | async-start | bytes 5242880 | tf_op jit(solution)/shard_map/all_to_all | solution.py:268
  290.3 342.3 %all-gather.11.cloned.1.call-start = ((), (), s32[]{:S(2)}) async-start(), calls=%async_computation.9 | async-start | bytes 13107200 | tf_op jit(solution)/shard_map/all_gather | solution.py:331
  314.4 30.2 %collective-permute-start.4 = (bf16[256,640]{1,0:T(8,128)(2,1)}, bf16[256,640]{1,0:T(8,128)(2,1)}, u32[]{:S(2)}, u32[]{:S(2)}) collective-permute-start(bf16[256,640]{1,0:T(8,128)(2,1)} %get-tuple-element.26), channel_id=1, source_target_pairs={{0,8},{8,16},{16,24},{24,0},{1,9},{9,17},{17,25},{25,1},{2,10},{10... | collective-permute-start | bytes 983048 | tf_op jit(solution)/shard_map/ppermute | solution.py:302
  315.8 30.8 %collective-permute-start.5 = (bf16[256,640]{1,0:T(8,128)(2,1)}, bf16[256,640]{1,0:T(8,128)(2,1)}, u32[]{:S(2)}, u32[]{:S(2)}) collective-permute-start(bf16[256,640]{1,0:T(8,128)(2,1)} %get-tuple-element.25), channel_id=1, source_target_pairs={{0,16},{8,24},{16,0},{24,8},{1,17},{9,25},{17,1},{25,9},{2,18},{10... | collective-permute-start | bytes 983048 | tf_op jit(solution)/shard_map/ppermute | solution.py:302
  318.4 28.2 %collective-permute-start.6 = (bf16[256,640]{1,0:T(8,128)(2,1)}, bf16[256,640]{1,0:T(8,128)(2,1)}, u32[]{:S(2)}, u32[]{:S(2)}) collective-permute-start(bf16[256,640]{1,0:T(8,128)(2,1)} %get-tuple-element.24), channel_id=1, source_target_pairs={{0,24},{8,0},{16,8},{24,16},{1,25},{9,1},{17,9},{25,17},{2,26},{10... | collective-permute-start | bytes 983048 | tf_op jit(solution)/shard_map/ppermute | solution.py:302
  341.2 5.1 copy-start.11
  343.4 10.7 %collective-permute-start.7 = (bf16[256,640]{1,0:T(8,128)(2,1)}, bf16[256,640]{1,0:T(8,128)(2,1)}, u32[]{:S(2)}, u32[]{:S(2)}) collective-permute-start(bf16[256,640]{1,0:T(8,128)(2,1)} %get-tuple-element.34), channel_id=1, source_target_pairs={{0,8},{8,16},{16,24},{24,0},{1,9},{9,17},{17,25},{25,1},{2,10},{10... | collective-permute-start | bytes 983048 | tf_op jit(solution)/shard_map/ppermute | solution.py:302
  343.9 15.0 %collective-permute-start.8 = (bf16[256,640]{1,0:T(8,128)(2,1)}, bf16[256,640]{1,0:T(8,128)(2,1)}, u32[]{:S(2)}, u32[]{:S(2)}) collective-permute-start(bf16[256,640]{1,0:T(8,128)(2,1)} %get-tuple-element.33), channel_id=1, source_target_pairs={{0,16},{8,24},{16,0},{24,8},{1,17},{9,25},{17,1},{25,9},{2,18},{10... | collective-permute-start | bytes 983048 | tf_op jit(solution)/shard_map/ppermute | solution.py:302
  344.7 16.2 %collective-permute-start.9 = (bf16[256,640]{1,0:T(8,128)(2,1)}, bf16[256,640]{1,0:T(8,128)(2,1)}, u32[]{:S(2)}, u32[]{:S(2)}) collective-permute-start(bf16[256,640]{1,0:T(8,128)(2,1)} %get-tuple-element.32), channel_id=1, source_target_pairs={{0,24},{8,0},{16,8},{24,16},{1,25},{9,1},{17,9},{25,17},{2,26},{10... | collective-permute-start | bytes 983048 | tf_op jit(solution)/shard_map/ppermute | solution.py:302
  363.4 2.6 copy-start.8
  381.2 1.5 copy-start.2
  382.7 31.2 %collective-permute-start.12 = (bf16[256,2560]{1,0:T(8,128)(2,1)S(1)}, bf16[256,2560]{1,0:T(8,128)(2,1)S(1)}, u32[]{:S(2)}, u32[]{:S(2)}) collective-permute-start(bf16[256,2560]{1,0:T(8,128)(2,1)S(1)} %get-tuple-element.14), channel_id=1, source_target_pairs={{0,8},{8,16},{16,24},{24,0},{1,9},{9,17},{17,25},{25,1},{2,10},{10... | collective-permute-start | bytes 3932168 | tf_op jit(solution)/shard_map/ppermute | solution.py:320
  384.1 30.9 %collective-permute-start.13 = (bf16[256,2560]{1,0:T(8,128)(2,1)S(1)}, bf16[256,2560]{1,0:T(8,128)(2,1)S(1)}, u32[]{:S(2)}, u32[]{:S(2)}) collective-permute-start(bf16[256,2560]{1,0:T(8,128)(2,1)S(1)} %get-tuple-element.13), channel_id=1, source_target_pairs={{0,24},{8,0},{16,8},{24,16},{1,25},{9,1},{17,9},{25,17},{2,26},{10... | collective-permute-start | bytes 3932168 | tf_op jit(solution)/shard_map/ppermute | solution.py:321
  466.4 56.8 %collective-permute-start.14 = (f32[256,2560]{1,0:T(8,128)}, f32[256,2560]{1,0:T(8,128)}, u32[]{:S(2)}, u32[]{:S(2)}) collective-permute-start(f32[256,2560]{1,0:T(8,128)} %get-tuple-element.11), channel_id=1, source_target_pairs={{0,24},{8,0},{16,8},{24,16},{1,25},{9,1},{17,9},{25,17},{2,26},{10... | collective-permute-start | bytes 7864328 | tf_op jit(solution)/shard_map/ppermute | solution.py:326
  468.3 57.9 %collective-permute-start.15 = (f32[256,2560]{1,0:T(8,128)}, f32[256,2560]{1,0:T(8,128)}, u32[]{:S(2)}, u32[]{:S(2)}) collective-permute-start(f32[256,2560]{1,0:T(8,128)} %get-tuple-element.12), channel_id=1, source_target_pairs={{0,8},{8,16},{16,24},{24,0},{1,9},{9,17},{17,25},{25,1},{2,10},{10... | collective-permute-start | bytes 7864328 | tf_op jit(solution)/shard_map/ppermute | solution.py:327
  490.3 35.9 %copy-start.3 = (bf16[512,2560]{1,0:T(8,128)(2,1)S(1)}, bf16[512,2560]{1,0:T(8,128)(2,1)}, u32[]{:S(2)}) copy-start(bf16[512,2560]{1,0:T(8,128)(2,1)} %copy-done.2) | copy-start | bytes 7864324
  632.7 8.9 %copy-start.1 = (bf16[640,2560]{1,0:T(8,128)(2,1)S(1)}, bf16[640,2560]{1,0:T(8,128)(2,1)}, u32[]{:S(2)}) copy-start(bf16[640,2560]{1,0:T(8,128)(2,1)} %param.17) | copy-start | bytes 9830404
Sparse Core Ops, SparseCore 0:
  9.5 115.3 all-gather.4
  126.4 82.8 all-gather.6
  210.9 106.2 all-gather.8
  533.3 99.3 all-gather.10
